TPU v7x, 32 devices: a whole 2x2x4 slice. The times are simulated.
32 devices in a mesh: section: 2 (over x), dp: 8 (over z, y), tensor: 2 (over core).
Axes of the slice: x: 2, y: 2, z: 4, core: 2. Of those that a mesh axis runs over, the one named last changes fastest.
Arguments:
- images: bfloat16 [128, 196, 512], P('dp', 'tensor'), may hold values from -6 to 6
- cotangent: bfloat16 [128, 196, 512], P('dp', 'tensor'), may hold values from -6 to 6
- norm1_gain: bfloat16 [2, 512], P('section', 'dp'), may hold values from 0.5 to 1.5
- norm1_bias: bfloat16 [2, 512], P('section', 'dp'), may hold values from -1.75 to 1.75
- qkv_weight: bfloat16 [2, 512, 3, 512], P('section', 'dp', None, 'tensor'), may hold values from -0.25 to 0.25
- qkv_bias: bfloat16 [2, 3, 512], P('section', None, ('tensor', 'dp')), may hold values from -1.75 to 1.75
- position_table: float32 [2, 169, 16], P('section', None, 'tensor'), may hold values from -6 to 6
- proj_weight: bfloat16 [2, 512, 512], P('section', ('tensor', 'dp')), may hold values from -0.75 to 0.75
- proj_bias: bfloat16 [2, 512], P('section', 'dp'), may hold values from -1.75 to 1.75
- norm2_gain: bfloat16 [2, 512], P('section', 'dp'), may hold values from 0.5 to 1.5
- norm2_bias: bfloat16 [2, 512], P('section', 'dp'), may hold values from -1.75 to 1.75
- fc1_weight: bfloat16 [2, 512, 2048], P('section', 'dp', 'tensor'), may hold values from -0.25 to 0.25
- fc1_bias: bfloat16 [2, 2048], P('section', ('tensor', 'dp')), may hold values from -1.75 to 1.75
- fc2_weight: bfloat16 [2, 2048, 512], P('section', ('tensor', 'dp')), may hold values from -0.125 to 0.125
- fc2_bias: bfloat16 [2, 512], P('section', 'dp'), may hold values from -1.75 to 1.75
Outputs:
- activations: bfloat16 [2, 128, 196, 512], P('section', 'dp', 'tensor')
- input_grad: bfloat16 [2, 128, 196, 512], P('section', 'dp', 'tensor')
- norm1_gain_grad: float32 [2, 512], P('section', 'dp')
- norm1_bias_grad: float32 [2, 512], P('section', 'dp')
- qkv_weight_grad: float32 [2, 512, 3, 512], P('section', 'dp', None, 'tensor')
- qkv_bias_grad: float32 [2, 3, 512], P('section', None, ('tensor', 'dp'))
- position_table_grad: float32 [2, 169, 16], P('section', None, 'tensor')
- proj_weight_grad: float32 [2, 512, 512], P('section', ('tensor', 'dp'))
- proj_bias_grad: float32 [2, 512], P('section', 'dp')
- norm2_gain_grad: float32 [2, 512], P('section', 'dp')
- norm2_bias_grad: float32 [2, 512], P('section', 'dp')
- fc1_weight_grad: float32 [2, 512, 2048], P('section', 'dp', 'tensor')
- fc1_bias_grad: float32 [2, 2048], P('section', ('tensor', 'dp'))
- fc2_weight_grad: float32 [2, 2048, 512], P('section', ('tensor', 'dp'))
- fc2_bias_grad: float32 [2, 512], P('section', 'dp')
All inputs are finite; a program needn't handle non-finite values.
Results may differ from a plain program's by a relative error of at most 0.023.
Values may be sent and summed in bfloat16 or wider, within the bound.
A program may use at most 256 MiB of HBM per device.

v0:
```python
import functools
import heapq
import math
import types

import jax
import jax.numpy as jnp
import numpy as np
from jax import lax
from jax.experimental import pallas as pl
from jax.experimental.pallas import tpu as pltpu
from jax.sharding import PartitionSpec as P

HEADS = 16
WIN = 7
SIDE = 14
SHIFT = 3

EPS = 1e-05
MASK_FILL = -100.0
ROOT_HALF = 0.7071067811865476
INV_ROOT_TWO_PI = 0.3989422804014327

ACROSS = SIDE // WIN
NW = ACROSS * ACROSS
WT = WIN * WIN
WP = 64
TABLE_SIDE = 2 * WIN - 1
CENTER = (WIN - 1) * TABLE_SIDE + WIN - 1
TABLE_PAD = 256
CH = 512
GATHER_ROWS = 16
BATCH = 2

SECTION = "section"
DP = "dp"
TENSOR = "tensor"

f32 = jnp.float32
bf16 = jnp.bfloat16
MESH = pl.DeviceIdType.MESH
NN = ((1,), (0,))
NT = ((1,), (1,))
TN = ((0,), (0,))


def round_up(n, m):
    return -(-n // m) * m


def window_slots(shift):
    slot = np.zeros(SIDE * SIDE, np.int64)
    for p in range(SIDE):
        for q in range(SIDE):
            token = ((p + shift) % SIDE) * SIDE + (q + shift) % SIDE
            window = (p // WIN) * ACROSS + q // WIN
            slot[token] = window * WP + (p % WIN) * WIN + q % WIN
    return slot


def window_permutation(parts, half, padded):
    perm = np.zeros((2, NW * WP, parts * padded), np.float32)
    for block in range(2):
        for token, slot in enumerate(window_slots(SHIFT * block)):
            perm[block, slot, (token // half) * padded + token % half] = 1
    return perm


def dotf(a, b, dims):
    return lax.dot_general(a, b, (dims, ((), ())), preferred_element_type=f32)


def normalize(values):
    center = values - jnp.mean(values, -1, keepdims=True)
    inverse = lax.rsqrt(jnp.mean(center * center, -1, keepdims=True) + EPS)
    return center * inverse, inverse


def norm_pull(upstream, normed, inverse, gain):
    scaled = upstream * gain
    return inverse * (
        scaled
        - jnp.mean(scaled, -1, keepdims=True)
        - normed * jnp.mean(scaled * normed, -1, keepdims=True)
    )


def block(i, n):
    if isinstance(i, int):
        return pl.ds(i * n, n)
    return pl.ds(pl.multiple_of(i * n, n), n)


def column_sum(v):
    return jnp.sum(v, 0, keepdims=True)


class Sizes:
    def __init__(self, mesh, images, fc1_weight):
        self.sections = mesh.shape[SECTION]
        self.dp = mesh.shape[DP]
        self.parts = mesh.shape[TENSOR]
        inner = int(math.isqrt(self.dp))
        while self.dp % inner:
            inner -= 1
        self.nb = inner
        self.na = self.dp // inner
        self.local_images, self.half, self.d = images.shape
        self.ff = fc1_weight.shape[-1] * self.parts
        self.ni = self.local_images // (self.sections * self.parts)
        self.hp = round_up(self.half, 8)
        self.rows = self.parts * self.hp
        self.m = self.ni * self.rows
        self.mw = self.ni * NW * WP
        self.hd = self.d // HEADS
        self.quad = 128 // self.hd
        self.ng = HEADS // self.quad
        self.nch = self.ff // CH
        self.scaling = self.hd**-0.5
        self.heads_part = HEADS // self.parts


LINK = 90.0e3
CORE_LINK = 430.0e3
HOP = 2.0
CORE_HOP = 0.8
MARGIN = 0.3
SKEW = 0.0
ZLAG = 0.0


class Plan:
    def __init__(self):
        self.clock = 0.0
        self.free = {}
        self.queue = []
        self.count = 0

    def link(self, name, size, rate, hop):
        begin = max(self.free.get(name, 0.0), self.clock)
        self.free[name] = begin + size / rate
        return begin + size / rate + hop + MARGIN

    def add(self, when, step):
        heapq.heappush(self.queue, (when, self.count, step))
        self.count += 1

    def pop(self):
        when, _, step = heapq.heappop(self.queue)
        self.clock = max(self.clock, when)
        step()

    def pop_of(self, wanted):
        found = [e for e in self.queue if isinstance(e[2], functools.partial) and wanted(e[2])]
        if found:
            entry = min(found)
            self.queue.remove(entry)
            heapq.heapify(self.queue)
            self.clock = max(self.clock, entry[0])
            entry[2]()
        return bool(found)

    def until(self, when):
        while self.queue and self.queue[0][0] <= when:
            self.pop()
        self.clock = max(self.clock, when)

    def due(self, when):
        return bool(self.queue) and self.queue[0][0] <= when


class Piece:
    def __init__(self, z, kind, index, rows, cols):
        self.kind, self.index, self.rows, self.cols = kind, index, rows, cols
        self.unit = rows * cols * 2 * z.parts

    def home(self, p):
        if self.kind == PROJ or (self.kind == QKV and self.index == 2):
            return None
        if self.kind == QKV:
            return p if self.index == 0 else 1 - p
        if p == 1 and self.index == 1:
            return None
        return p if self.kind == FC1 else 1 - p

    def sum_home(self, p):
        if self.index == 1 and self.kind in (FC1, FC2):
            return 0 if self.kind == FC1 else 1
        return None


QKV, PROJ, FC1, FC2 = range(4)


def make_pieces(z, qrow, prow, f2row):
    pieces = [Piece(z, QKV, k, qrow, z.d // z.parts) for k in range(3)]
    pieces.append(Piece(z, PROJ, 0, prow, z.d))
    pieces += [Piece(z, FC1, k, qrow, z.ff // z.parts // 2) for k in range(2)]
    pieces += [Piece(z, FC2, k, f2row // 2, z.d) for k in range(2)]
    for i, piece in enumerate(pieces):
        piece.id = i
    return pieces


def kernel(z, *refs):
    r = types.SimpleNamespace(**dict(zip(z.names, refs)))
    s = lax.axis_index(SECTION)
    d = lax.axis_index(DP)
    t = lax.axis_index(TENSOR)
    na, nb, nt, ns, ni = z.na, z.nb, z.parts, z.sections, z.ni
    a = d // nb
    b = lax.rem(d, nb)
    rows, m = z.rows, z.m
    pieces = z.pieces
    plan = Plan()

    def dev(s_=None, a_=None, b_=None, t_=None):
        s_ = s if s_ is None else s_
        a_ = a if a_ is None else a_
        b_ = b if b_ is None else b_
        t_ = t if t_ is None else t_
        return (s_, a_ * nb + b_, t_)

    def ahead(base, n):
        return [lax.rem(base + k, n) for k in range(1, n)]

    def behind(base, n):
        return [lax.rem(base + n - k, n) for k in range(1, n)]

    x_peers, x_from = ahead(s, ns), behind(s, ns)
    a_peers, a_from = ahead(a, na), behind(a, na)
    b_peers, b_from = ahead(b, nb), behind(b, nb)
    c_peers, c_from = ahead(t, nt), behind(t, nt)
    ALL = slice(None)

    def win(q, ref, lead, a_, b_, t_):
        if q.kind == QKV:
            return ref.at[lead + (q.index, t_, a_, b_)]
        if q.kind == FC1:
            return ref.at[lead + (t_, q.index, a_, b_)]
        if q.kind == FC2:
            return ref.at[lead + (t_, a_, b_, pl.ds(q.index * q.rows, q.rows))]
        return ref.at[lead + (t_, a_, b_)]

    wref = {QKV: r.wq, PROJ: r.wp, FC1: r.w1, FC2: r.w2}

    def shard(q, q_ref, p_ref, f1_ref, f2_ref):
        if q.kind == QKV:
            return q_ref.at[q.index]
        if q.kind == FC1:
            return f1_ref.at[:, pl.ds(q.index * q.cols, q.cols)]
        if q.kind == FC2:
            return f2_ref.at[pl.ds(q.index * q.rows, q.rows)]
        return p_ref

    lx, xs = r.lx, r.xs
    zs, zr, ys, yr, cs, cr = r.zs, r.zr, r.ys, r.yr, r.cs, r.cr

    def remote(src, dst, ss, rs, device):
        return pltpu.make_async_remote_copy(
            src_ref=src, dst_ref=dst, send_sem=ss, recv_sem=rs, device_id=device, device_id_type=MESH
        )

    def send(src, dst, ss, rs, device):
        remote(src, dst, ss, rs, device).start()

    def arrived(dst, sem):
        pltpu.make_async_copy(dst, dst, sem).wait()

    ready_at, x_at = {}, {}
    steps_left = {}

    def planes(home):
        return range(ns) if home is None else (home,)

    def on(home, body):
        if home is None:
            body()
        else:
            pl.when(s == home)(body)

    def other(home):
        return 1 - home

    def own_shard(q):
        return shard(q, r.q_in, r.p_in, r.f1_in, r.f2_in)

    def start_x(q):
        for p in range(ns):
            home = q.home(p)
            target = win(q, wref[q.kind], (p,), a, b, t)

            @pl.when(s == p)
            def _():
                if home in (None, p):
                    pltpu.make_async_copy(own_shard(q), target, lx.at[q.id, p]).start()
                if home != p:
                    send(own_shard(q), target, xs.at[q.id], lx.at[q.id, p], dev(s_=other(p)))

            x_at[q.id, p] = plan.clock + 1.0
            if home != p:
                x_at[q.id, p] = plan.link(f"x{p}", q.unit, LINK, HOP)
            steps_left[q.id, p] = na if home is None else 2 * na

    def link_of(name, home, size):
        return max(plan.link(f"{name}{h}", size, LINK, HOP) for h in planes(home))

    def go_z(q, p):
        here = win(q, wref[q.kind], (p,), a, b, t)
        home = q.home(p)
        plan.clock = max(plan.clock, x_at[q.id, p])

        def body():
            arrived(here, lx.at[q.id, p])
            for k, peer in enumerate(a_peers):
                send(here, here, zs.at[q.id, p, k], zr.at[q.id, p, k], dev(a_=peer))

        on(home, body)
        plan.add(plan.clock, functools.partial(go_y, q, p, 0))
        for k in range(na - 1):
            when = link_of("z", home, q.unit * na / (na - 1))
            plan.add(when + ZLAG * p, functools.partial(go_y, q, p, k + 1))

    def source_row(k):
        return a if k == 0 else a_from[k - 1]

    def go_y(q, p, k):
        here = win(q, wref[q.kind], (p,), source_row(k), b, t)
        home = q.home(p)

        def body():
            if k:
                arrived(here, zr.at[q.id, p, k - 1])
            for j, peer in enumerate(b_peers):
                send(here, here, ys.at[q.id, p, k, j], yr.at[q.id, p, k, j], dev(b_=peer))

        on(home, body)
        for j in range(nb - 1):
            when = link_of("y", home, q.unit)
        plan.add(when, functools.partial(go_c, q, p, k))

    def to_core(q, p, k):
        here = win(q, wref[q.kind], (p,), source_row(k), ALL, t)
        for j, peer in enumerate(c_peers):
            send(here, here, cs.at[q.id, p, k, j], cr.at[q.id, p, k, j], dev(t_=peer))

    def core_time(q, p):
        when = plan.link("c", q.unit * nb / nt, CORE_LINK, CORE_HOP)
        ready_at[q.id, p] = max(when, ready_at.get((q.id, p), 0.0))
        steps_left[q.id, p] -= 1

    def go_c(q, p, k):
        home = q.home(p)

        def body():
            for j, source in enumerate(b_from):
                arrived(win(q, wref[q.kind], (p,), source_row(k), source, t), yr.at[q.id, p, k, j])
            if home is not None:
                here = win(q, wref[q.kind], (p,), source_row(k), ALL, t)
                send(here, here, r.ws.at[q.id, p, k], r.wr.at[q.id, p, k], dev(s_=other(home)))
            to_core(q, p, k)

        on(home, body)
        core_time(q, p)
        if home is not None:
            when = plan.link(f"x{home}", q.unit * nb, LINK, HOP)
            plan.add(when, functools.partial(go_w, q, p, k))

    def go_w(q, p, k):
        def body():
            arrived(win(q, wref[q.kind], (p,), source_row(k), ALL, t), r.wr.at[q.id, p, k])
            to_core(q, p, k)

        on(other(q.home(p)), body)
        core_time(q, p)

    def concerns(group, p, step):
        args = getattr(step, "args", ())
        if step.func is next_z:
            return any(q in group and e == p for q, e in order[args[0] :])
        return len(args) > 1 and args[1] == p and args[0] in group

    def need(kind, p, index=None):
        group = [q for q in pieces if q.kind == kind or (kind == FC1 and q.kind == FC2)]
        mine = [q for q in pieces if q.kind == kind and index in (None, q.index)]
        while any(steps_left[q.id, p] for q in mine):
            plan.pop()
        for q in mine:
            plan.clock = max(plan.clock, ready_at[q.id, p])
            for k in range(na):
                for j, source in enumerate(c_from):
                    arrived(win(q, wref[q.kind], (p,), source_row(k), ALL, source), cr.at[q.id, p, k, j])

    def gather_sent():
        for q in pieces:
            for p in range(ns):
                home = q.home(p)
                here = win(q, wref[q.kind], (p,), a, b, t)

                if home != p:

                    @pl.when(s == p)
                    def _():
                        arrived(own_shard(q), xs.at[q.id])

                def plane():
                    for k in range(na - 1):
                        arrived(here, zs.at[q.id, p, k])
                    for k in range(na):
                        for j in range(nb - 1):
                            arrived(here, ys.at[q.id, p, k, j])
                        if home is not None:
                            arrived(win(q, wref[q.kind], (p,), a, ALL, t), r.ws.at[q.id, p, k])

                on(home, plane)
                for k in range(na):
                    for j in range(nt - 1):
                        arrived(win(q, wref[q.kind], (p,), a, ALL, t), cs.at[q.id, p, k, j])

    def run(lo, hi, cost, body, before=None):
        def one(i, carry):
            for k in range(lo, hi):
                if before is not None or plan.due(plan.clock):

                    @pl.when(i == k)
                    def _():
                        plan.until(plan.clock)
                        if before is not None:
                            before(k)

                plan.clock += cost

            body(i)
            return carry

        lax.fori_loop(lo, hi, one, 0)
        plan.until(plan.clock)

    def spent(cost):
        plan.until(plan.clock + cost)

    SMF = r.smf
    P0, P1, P2 = r.p0, r.p1, r.p2
    small_ready = []

    def small_start():
        P0[s] = r.sm_in[...]
        for k, peer in enumerate(x_peers):
            send(r.sm_in, P0.at[s], r.ps.at[0, k], r.psr.at[0, k], dev(s_=peer))
        plan.add(plan.link("x0", P0.size * nt, LINK, HOP), small_a)

    def small_part(src, dst, level, targets):
        for k, target in enumerate(targets):
            send(src, dst.at[k], r.ps.at[level, k], r.psr.at[level, k], target)

    def small_sum(base, takes, level):
        total = base[...].astype(f32)
        for k in range(takes.shape[0]):
            arrived(takes.at[k], r.psr.at[level, k])
            total = total + takes[k].astype(f32)
        return total

    def small_a():
        for k, source in enumerate(x_from):
            arrived(P0.at[source], r.psr.at[0, k])
        small_part(P0, r.pa, 1, [dev(a_=p) for p in a_peers])
        for h in range(ns):
            when = plan.link(f"z{h}", P0.size * 2 * nt * na + SKEW * LINK, LINK, HOP)
        plan.add(when, small_b)

    def small_b():
        P1[...] = small_sum(P0, r.pa, 1).astype(bf16)
        small_part(P1, r.pb, 2, [dev(b_=p) for p in b_peers])
        plan.add(plan.link("y0", P0.size * 2 * nt, LINK, HOP), small_c)

    def small_c():
        P2[...] = small_sum(P1, r.pb, 2).astype(bf16)
        small_part(P2, r.pc, 3, [dev(t_=p) for p in c_peers])
        plan.add(plan.clock + CORE_HOP, small_d)

    def small_d():
        SMF[...] = small_sum(P2, r.pc, 3)
        small_ready.append(True)

    def need_small():
        while not small_ready:
            plan.pop()

    def small_sent():
        arrived(r.sm_in, r.ps.at[0, 0])
        for level, takes in ((1, r.pa), (2, r.pb), (3, r.pc)):
            for k in range(takes.shape[0]):
                arrived(takes.at[k], r.ps.at[level, k])

    group = s * nt + t

    def group_images(g):
        return pl.ds(g * ni, ni)

    barrier = pltpu.get_barrier_semaphore()
    peers = (
        [dev(a_=p) for p in a_peers]
        + [dev(b_=p) for p in b_peers]
        + [dev(t_=p) for p in c_peers]
        + [dev(s_=p) for p in x_peers]
        + [dev(s_=p, t_=q) for p in x_peers for q in c_peers]
    )
    for p in peers:
        pl.semaphore_signal(barrier, inc=1, device_id=p, device_id_type=MESH)
    pl.semaphore_wait(barrier, len(peers))

    tbl = r.tbl
    pltpu.make_async_copy(r.tbl_in, tbl.at[s, t], r.tx.at[s]).start()
    for k, peer in enumerate(x_peers):
        send(r.tbl_in, tbl.at[s, t], r.txs.at[k], r.tx.at[s], dev(s_=peer))
    small_start()
    for q in pieces:
        start_x(q)
    xin = r.outb
    for j, src in enumerate((r.images, r.cotangent)):
        pltpu.make_async_copy(src.at[group_images(group)], xin.at[j, t], r.xl.at[j]).start()
        for k, peer in enumerate(c_peers):
            send(
                src.at[group_images(s * nt + peer)],
                xin.at[j, t],
                r.xcs.at[j, k],
                r.xcr.at[j, k],
                dev(t_=peer),
            )

    def image_ready(j):
        arrived(xin.at[j, t], r.xl.at[j])
        for k, source in enumerate(c_from):
            arrived(xin.at[j, source], r.xcr.at[j, k])

    pad_rows = jnp.zeros((z.hp - z.half, z.d), f32)

    def load_rows(j, ref):
        def one(i, _):
            pieces = []
            for h in range(nt):
                pieces.append(xin[j, h, i].astype(f32))
                if z.hp > z.half:
                    pieces.append(pad_rows)
            ref[block(i, rows), :] = jnp.concatenate(pieces, 0).astype(ref.dtype)
            return 0

        lax.fori_loop(0, ni, one, 0)

    outb = r.outb

    ships = {}

    def ship(kind, p, slot, i):
        out = r.act if kind == 0 else r.ig
        for h in range(nt):
            target = out.at[group * ni + i]
            mine = jnp.logical_and(s == p, t == h)

            @pl.when(mine)
            def _():
                pltpu.make_async_copy(outb.at[slot, h, i], target, r.os.at[kind, p, h]).start()

            @pl.when(jnp.logical_not(mine))
            def _():
                remote(
                    outb.at[slot, h, i], target, r.os.at[kind, p, h], r.orr.at[kind, group], (p, d, h)
                ).start()

        plan.link(f"x{other(p)}", rows * z.d * 2 * nt, LINK, HOP)
        ships[kind, p] = ships.get((kind, p), 0) + 1

    def ship_later(kind, p, slot, times):
        for i in range(ni):
            plan.add(plan.clock + times[i % len(times)], functools.partial(ship, kind, p, slot, i))

    def shipped(kind, p, slot):
        while ships.get((kind, p), 0) < ni:
            plan.pop()
        for h in range(nt):
            arrived(outb.at[slot, h], r.os.at[kind, p, h])

    def received(kind):
        out = r.act if kind == 0 else r.ig
        for g in range(ns * nt):

            @pl.when(g != group)
            def _():
                arrived(out.at[group_images(g)], r.orr.at[kind, g])

    def stage_out(value, i, slot):
        for h in range(nt):
            outb[slot, h, i] = value[h * z.hp : h * z.hp + z.half].astype(bf16)

    width = z.d // nt

    def w_qkv(p, c, part):
        return r.wq[p, c, part].reshape(z.d, width)

    def q_part(part):
        return slice(part * width, (part + 1) * width)

    def w_proj(p):
        return r.wp[p].reshape(z.d, z.d)

    w1_all = r.w1.reshape(2, z.nch, na, nb, r.w1.shape[-2], CH)

    def w_fc1(p, c):
        return w1_all[p, c].reshape(z.d, CH)

    w2_per = CH // r.w2.shape[-2]
    w2_all = r.w2.reshape(2, z.nch, w2_per, r.w2.shape[-2], z.d)

    def w_fc2(p, c):
        return w2_all[p, c].reshape(CH, z.d)

    def row(p, k):
        return SMF[p, pl.ds(k, 1), :]

    def masks(dtype):
        lane = lax.broadcasted_iota(jnp.int32, (WP, 128), 1) // z.hd
        return [(lane == h).astype(dtype) for h in range(z.quad)]

    def spread(v, mk):
        return jnp.concatenate([v * q for q in mk], 0)

    def collect(v, mk):
        acc = v[0:WP] * mk[0]
        for h in range(1, z.quad):
            acc = acc + v[h * WP : (h + 1) * WP] * mk[h]
        return acc

    BM = r.bm
    lanes = 128
    per_lane = lanes // WP

    def build_bias(p):
        j = lax.broadcasted_iota(jnp.int32, (WP, lanes), 0)
        lane = lax.broadcasted_iota(jnp.int32, (WP, lanes), 1)
        i = lax.rem(lane, WP)
        iy, ix, jy, jx = i // WIN, lax.rem(i, WIN), j // WIN, lax.rem(j, WIN)
        valid = jnp.logical_and(i < WT, j < WT)
        index = (iy - jy + WIN - 1) * TABLE_SIDE + ix - jx + WIN - 1
        index = jnp.where(valid, index, 0)
        low = jnp.where(index < lanes, index, 0)
        high = jnp.where(index < lanes, 0, index - lanes)
        head_of_lane = lane // WP
        tables = tbl.reshape(2, HEADS, TABLE_PAD)

        def look(head):
            entry = tables[p, pl.ds(head, 1), :]
            one = jnp.take_along_axis(jnp.broadcast_to(entry[:, :lanes], (WP, lanes)), low, axis=1)
            two = jnp.take_along_axis(jnp.broadcast_to(entry[:, lanes:], (WP, lanes)), high, axis=1)
            return jnp.where(index < lanes, one, two)

        def region(q, wy):
            first = jnp.zeros_like(q)
            if wy < ACROSS - 1:
                return first
            return jnp.where(q < WIN - SHIFT, first + 1, first + 2)

        def group_of_heads(g, carry):
            for c in range(z.quad // per_lane):
                value = look(g * z.quad + c * per_lane)
                for e in range(1, per_lane):
                    value = jnp.where(head_of_lane == e, look(g * z.quad + c * per_lane + e), value)
                value = jnp.where(j < WT, value, -1e30)
                for w in range(NW if p else 1):
                    out = value
                    if p == 1:
                        wy, wx = w // ACROSS, w % ACROSS
                        label_i = region(iy, wy) * 3 + region(ix, wx)
                        label_j = region(jy, wy) * 3 + region(jx, wx)
                        out = out + jnp.where(
                            jnp.logical_and(valid, label_i != label_j), MASK_FILL, 0.0
                        )
                    BM[p + w, g, :, c * lanes : (c + 1) * lanes] = out
            return carry

        lax.fori_loop(0, z.ng, group_of_heads, 0)

    X, G = r.mg, r.g
    PM, PMT = r.pm, r.pmt
    FN, N1, K = r.fn, r.n1, r.k
    QK, PR, CTX, CTXT = r.qk, r.pr, r.ctx, r.ctxt
    MID, MG, SN, N2, ACT, SL = r.mid, r.mg, r.sn, r.n2, r.actv, r.sl
    SG, DB = r.sg, r.db

    def forward(p):
        need_small()

        def ln1(i):
            n, inv = normalize(X[block(i, rows), :])
            N1[p, block(i, rows), :] = n.astype(bf16)
            K[block(i, rows), 2 * p : 2 * p + 1] = inv
            f = (n * row(p, 0) + row(p, 1)).astype(bf16)
            FN[p, block(i, rows), :] = f
            CTX[block(i, NW * WP), :] = dotf(PM[p], f, NN).astype(bf16)

        run(0, ni, 0.45, ln1)

        def qkv(c):
            for e in range(nt):
                bias = row(p, 6 + c)[:, q_part(e)]
                QK[p, c, :, q_part(e)] = (dotf(CTX[...], w_qkv(p, c, e), NN) + bias).astype(bf16)

        need(QKV, p)
        run(0, 3, 0.7, qkv)

        def attention(i):
            mb, mf = masks(bf16), masks(f32)
            units = [(i * BATCH + e, g) for e in range(BATCH) for g in range(z.ng)]
            at = [(block(u, WP), slice(g * 128, (g + 1) * 128)) for u, g in units]
            raw = [dotf(QK[p, 1, S, L], spread(QK[p, 0, S, L], mb), NT) for S, L in at]
            prs = []
            for (u, g), sc in zip(units, raw):
                w = 1 + lax.rem(u, NW) if p else 0
                sc = sc * z.scaling + BM[w, g]
                e = jnp.exp(sc - jnp.max(sc, 0, keepdims=True))
                pr = (e * (1.0 / jnp.sum(e, 0, keepdims=True))).astype(bf16)
                PR[p, u, g] = pr
                prs.append(pr)
            mixed = [dotf(pr, QK[p, 2, S, L], TN) for pr, (S, L) in zip(prs, at)]
            for v, (S, L) in zip(mixed, at):
                CTX[S, L] = collect(v, mf).astype(bf16)

        run(0, ni * NW // BATCH, 0.72, attention)

        def unperm(i):
            CTXT[p, block(i, rows), :] = dotf(PMT[p], CTX[block(i, NW * WP), :], NN).astype(bf16)

        run(0, ni, 0.21, unperm)
        need(PROJ, p)
        MID[...] = dotf(CTXT[p], w_proj(p), NN)
        spent(0.6)

        def ln2(i):
            mid = X[block(i, rows), :] + MID[block(i, rows), :] + row(p, 2)
            MID[block(i, rows), :] = mid
            n, inv = normalize(mid)
            N2[p, block(i, rows), :] = n.astype(bf16)
            K[block(i, rows), 2 * p + 1 : 2 * p + 2] = inv
            SN[p, block(i, rows), :] = (n * row(p, 3) + row(p, 4)).astype(bf16)

        run(0, ni, 0.26, ln2)
        if p == 1:
            for j, ref in enumerate((ACT, SL)):
                arrived(ref, r.sp.at[j])
        per = z.nch // 2

        for j in range(2):
            need(FC1, p, j)

            def rise(i):
                c = j + 2 * i
                u = dotf(SN[p], w_fc1(p, c), NN) + row(p, 9 + c)
                e = 0.5 * (1.0 + lax.erf(u * ROOT_HALF))
                ACT[c] = (u * e).astype(bf16)
                SL[c] = (e + u * jnp.exp(-0.5 * u * u) * INV_ROOT_TWO_PI).astype(bf16)

            run(0, per, 1.16, rise)
        need(FC2, p)

        def fall(c):
            MID[...] += dotf(ACT[c], w_fc2(p, c), NN)

        run(0, z.nch, 0.6, fall)
        if p == 0:
            for j, ref in enumerate((ACT, SL)):
                pltpu.make_async_copy(ref, r.spill.at[j], r.sp.at[j]).start()

        def finish(i):
            value = MID[block(i, rows), :] + row(p, 5)
            X[block(i, rows), :] = value.astype(bf16).astype(f32)
            stage_out(value, i, p)

        run(0, ni, 0.05, finish)
        ship_later(0, p, p, (9.0, 14.0, 19.0, 24.0) if p == 0 else (0.0, 5.0, 10.0, 15.0))

    g1_own = r.g1.reshape(z.nch, *w1_all.shape[2:])
    g2_own = r.g2.reshape(z.nch, *w2_all.shape[2:])

    def backward(p):
        gq, gp, g1, g2 = (
            (r.gq, r.gp, g1_own, g2_own) if p else (r.wq.at[1], r.wp.at[1], w1_all.at[1], w2_all.at[1])
        )
        def addrow(k, v):
            SG[p, pl.ds(k, 1), 0 : z.d] = SG[p, pl.ds(k, 1), 0 : z.d] + v

        SG[p] = jnp.zeros(SG.shape[1:], f32)
        DB[...] = jnp.zeros(DB.shape, f32)
        if p == 0:
            for j, ref in enumerate((ACT, SL)):
                arrived(ref, r.sp.at[j])
            gather_sent()

        def fc2_grad(c):
            g2[c] = dotf(ACT[c], G[...], TN).astype(bf16).reshape(g2.shape[1:])

        run(0, z.nch, 0.62, fc2_grad)
        emit(FC2, p)

        def hidden(c):
            hg = dotf(G[...], w_fc2(p, c), NT) * SL[c].astype(f32)
            SG[p, pl.ds(9 + c, 1), 0 : z.d] = column_sum(hg)
            SL[c] = hg.astype(bf16)

        run(0, z.nch, 0.65, hidden)

        def fc1(c):
            g1[c] = dotf(SN[p], SL[c], TN).astype(bf16).reshape(g1.shape[1:])

        run(0, z.nch, 0.75, fc1)
        MID[...] = jnp.zeros(MID.shape, f32)
        emit(FC1, p)

        def n2g(c):
            MID[...] += dotf(SL[c], w_fc1(p, c), NT)

        run(0, z.nch, 0.65, n2g)
        if p == 1:
            for j, ref in enumerate((ACT, SL)):
                pltpu.make_async_copy(r.spill.at[j], ref, r.sp.at[j]).start()

        def ln2(i):
            sl = block(i, rows)
            ng = MID[sl, :]
            n = N2[p, sl, :].astype(f32)
            g = G[sl, :].astype(f32)
            mg = g + norm_pull(ng, n, K[sl, 2 * p + 1 : 2 * p + 2], row(p, 3))
            MG[sl, :] = mg
            addrow(5, column_sum(g))
            addrow(3, column_sum(ng * n))
            addrow(4, column_sum(ng))
            addrow(2, column_sum(mg))
            G[sl, :] = mg.astype(bf16)

        run(0, ni, 0.31, ln2)
        gp[...] = dotf(CTXT[p], G[...], TN).astype(bf16).reshape(gp.shape)
        CTXT[p] = dotf(G[...], w_proj(p), NT).astype(bf16)
        spent(1.2)

        def cgrad(i):
            CTX[block(i, NW * WP), :] = dotf(PM[p], CTXT[p, block(i, rows), :], NN).astype(bf16)

        run(0, ni, 0.23, cgrad)
        emit(PROJ, p)

        def attention(i):
            mb, mf = masks(bf16), masks(f32)
            units = [(i * BATCH + e, g) for e in range(BATCH) for g in range(z.ng)]
            at = [(block(u, WP), slice(g * 128, (g + 1) * 128)) for u, g in units]
            cbd = [spread(CTX[S, L], mb) for S, L in at]
            dps = [dotf(QK[p, 2, S, L], c, NT) for (S, L), c in zip(at, cbd)]
            dvs = [dotf(PR[p, u, g], c, NN) for (u, g), c in zip(units, cbd)]
            sbs = []
            for (u, g), dp in zip(units, dps):
                pf = PR[p, u, g].astype(f32)
                tt = pf * dp
                sc = tt - pf * jnp.sum(tt, 0, keepdims=True)
                DB[g] = DB[g] + sc
                sbs.append(sc.astype(bf16))
            for v, (S, L) in zip(dvs, at):
                QK[p, 2, S, L] = v.astype(bf16)
            dks = [dotf(sb, spread(QK[p, 0, S, L], mb), NN) for sb, (S, L) in zip(sbs, at)]
            dqs = [dotf(sb, QK[p, 1, S, L], TN) for sb, (S, L) in zip(sbs, at)]
            for dk, dq, (S, L) in zip(dks, dqs, at):
                QK[p, 1, S, L] = (dk * z.scaling).astype(bf16)
                QK[p, 0, S, L] = (collect(dq, mf) * z.scaling).astype(bf16)

        def un(c, i):
            dv = dotf(PMT[p], QK[p, c, block(i, NW * WP), :], NN)
            addrow(6 + c, column_sum(dv))
            QK[p, c, block(i, rows), :] = dv.astype(bf16)

        def qkv_grad(c):
            value = dotf(FN[p], QK[p, c, 0:m, :], TN).astype(bf16)
            for e in range(nt):
                gq[c, e] = value[:, q_part(e)].reshape(gq.shape[2:])

        def emit_last(k):
            if k:
                emit(QKV, p, k - 1)

        def pull(sl, c):
            return sum(dotf(QK[p, c, sl, q_part(e)], w_qkv(p, c, e), NT) for e in range(nt))

        def ln1(i):
            sl = block(i, rows)
            ng = pull(sl, 0) + pull(sl, 1) + pull(sl, 2)
            n = N1[p, sl, :].astype(f32)
            xg = MG[sl, :] + norm_pull(ng, n, K[sl, 2 * p : 2 * p + 1], row(p, 0))
            addrow(0, column_sum(ng * n))
            addrow(1, column_sum(ng))
            if p:
                G[sl, :] = xg.astype(bf16)
            stage_out(xg, i, 1 - p)

        shipped(0, 1 - p, 1 - p)
        per = NW // BATCH
        cost = 1.6

        def image_step(k):
            attention(k)

            @pl.when(lax.rem(k, per) == per - 1)
            def _():
                for c in range(3):
                    un(c, k // per)
                ln1(k // per)

        first = per * cost
        if p == 0:
            ship_later(1, p, 1 - p, [first * (i + 1) for i in range(ni)])
        else:
            ship_later(1, p, 1 - p, [first * ni + 4.0 + 5.0 * i for i in range(ni)])
        run(0, ni * per, cost, image_step)
        run(0, 3, 0.75, qkv_grad, emit_last)
        emit(QKV, p, 2)
        table_rows(p)
        sum_send(p, 0)

    def table_rows(p):
        src = lax.broadcasted_iota(jnp.int32, (z.quad * WP, TABLE_PAD), 0)
        dst = lax.broadcasted_iota(jnp.int32, (z.quad * WP, TABLE_PAD), 1)
        i = lax.rem(src, WP)
        place = jnp.logical_and(
            i < WT, dst == CENTER - ((i // WIN) * TABLE_SIDE + lax.rem(i, WIN))
        )
        head = src // WP
        pick = jnp.concatenate(
            [jnp.logical_and(place, head == h).astype(bf16) for h in range(z.quad)], 1
        )
        group_row = lax.broadcasted_iota(jnp.int32, (8, WP), 0)
        group_of = lax.broadcasted_iota(jnp.int32, (8, WP), 1)
        rows_of = jnp.logical_and(group_of < WT, group_of // WIN == group_row).astype(bf16)

        def split_dot(x, y, left):
            big = x if left else y
            hi = big.astype(bf16)
            lo = (big - hi.astype(f32)).astype(bf16)
            if left:
                return dotf(hi, y, NN) + dotf(lo, y, NN)
            return dotf(x, hi, NN) + dotf(x, lo, NN)

        def one_group(g):
            e = split_dot(DB[g], pick, True)
            for h in range(z.quad):
                v = e[:, h * TABLE_PAD : (h + 1) * TABLE_PAD]
                v = pltpu.roll(v, 0, 1, stride=1, stride_axis=0)
                v = split_dot(rows_of, v, False)
                v = pltpu.roll(v, 0, 1, stride=TABLE_SIDE - WIN, stride_axis=0)
                SG[p, pl.ds(g * z.quad + h, 1), z.d :] = column_sum(v)

        run(0, z.ng, 0.4, one_group)

    gref = {QKV: r.gq, PROJ: r.gp, FC1: r.g1, FC2: r.g2}
    s1, v1, s2, v2, s3, v3, s4, v4 = (r.s1, r.v1, r.s2, r.v2, r.s3, r.v3, r.s4, r.v4)
    k1, k2, k3 = r.k1, r.k2, r.k3
    done = {}

    def buffer(level, q):
        return getattr(r, f"r{level}_{q.id}")

    def gwin(q, p, a_, b_, t_):
        if p == 0:
            return win(q, wref[q.kind], (1,), a_, b_, t_)
        return win(q, gref[q.kind], (), a_, b_, t_)

    def gout(q):
        return shard(q, r.gq_out, r.gp_out, r.g1_out, r.g2_out)

    def reached(q, p, level):
        while done.get((q.id, p), 0) < level:
            plan.pop()

    def credit(sem, q, k, p, device):
        if p == 1:
            pl.semaphore_signal(sem.at[q.id, k], inc=1, device_id=device, device_id_type=MESH)

    def spend(sem, q, k, p):
        if p == 0:
            pl.semaphore_wait(sem.at[q.id, k], 1)

    def emit(kind, p, index=None):
        for q in pieces:
            if q.kind == kind and index in (None, q.index):
                r1(q, p)

    def r1(q, p):
        if p == 0:
            reached(q, 1, 2)
        for k, peer in enumerate(c_peers):
            spend(k1, q, k, p)
            send(gwin(q, p, ALL, ALL, peer), buffer(1, q).at[k], s1.at[p, q.id, k], v1.at[p, q.id, k], dev(t_=peer))
            when = plan.link("c", q.unit * na * nb / nt, CORE_LINK, CORE_HOP)
        done[q.id, p] = 1
        plan.add(when, functools.partial(r2, q, p))

    def r2(q, p):
        if p == 0:
            reached(q, 1, 3)
        for k in range(nt - 1):
            arrived(buffer(1, q).at[k], v1.at[p, q.id, k])
        mine = gwin(q, p, ALL, ALL, t)
        add_into(mine, [buffer(1, q).at[k] for k in range(nt - 1)])
        for k, source in enumerate(c_from):
            credit(k1, q, k, p, dev(t_=source))
        plan.clock += q.unit * na * nb / 10e6
        done[q.id, p] = 2
        home = q.sum_home(p)
        if home is None:
            to_y(q, p)
            return

        @pl.when(s != home)
        def _():
            spend(r.k6, q, 0, p)
            send(mine, buffer(6, q), r.s6.at[p, q.id], r.v6.at[p, q.id], dev(s_=home))

        when = plan.link(f"x{other(home)}", q.unit * na * nb, LINK, HOP)
        plan.add(when, functools.partial(r2x, q, p))

    def r2x(q, p):
        home = q.sum_home(p)

        def body():
            arrived(buffer(6, q), r.v6.at[p, q.id])
            add_into(gwin(q, p, ALL, ALL, t), [buffer(6, q)])
            credit(r.k6, q, 0, p, dev(s_=other(home)))

        on(home, body)
        plan.clock += q.unit * na * nb / 10e6
        to_y(q, p)

    def to_y(q, p):
        home = q.sum_home(p)

        def body():
            for k, peer in enumerate(b_peers):
                spend(k2, q, k, p)
                send(
                    gwin(q, p, ALL, peer, t),
                    buffer(2, q).at[k],
                    s2.at[p, q.id, k],
                    v2.at[p, q.id, k],
                    dev(b_=peer),
                )

        on(home, body)
        for k in range(nb - 1):
            when = link_of("y", home, q.unit * na)
        plan.add(when, functools.partial(r3, q, p))

    def r3(q, p):
        if p == 0:
            reached(q, 1, 4)
        home = q.sum_home(p)

        def body():
            for k in range(nb - 1):
                arrived(buffer(2, q).at[k], v2.at[p, q.id, k])
            add_into(gwin(q, p, ALL, b, t), [buffer(2, q).at[k] for k in range(nb - 1)])
            for k, source in enumerate(b_from):
                credit(k2, q, k, p, dev(b_=source))
            for k, peer in enumerate(a_peers):
                spend(k3, q, k, p)
                send(
                    gwin(q, p, peer, b, t),
                    buffer(3, q).at[k],
                    s3.at[p, q.id, k],
                    v3.at[p, q.id, k],
                    dev(a_=peer),
                )

        on(home, body)
        for k in range(na - 1):
            when = link_of("z", home, q.unit * na / (na - 1))
        done[q.id, p] = 3
        plan.add(when, functools.partial(r4, q, p))

    def r4(q, p):
        if p == 0:
            reached(q, 1, 5)
        home = q.sum_home(p)
        mine = gwin(q, p, a, b, t)

        def summed():
            for k in range(na - 1):
                arrived(buffer(3, q).at[k], v3.at[p, q.id, k])
            total = mine[...].astype(f32)
            for k in range(na - 1):
                total = total + buffer(3, q)[k].astype(f32)
            for k, source in enumerate(a_from):
                credit(k3, q, k, p, dev(a_=source))
            return total

        def keep(total):
            gout(q)[...] = total

        def pass_on(total):
            buffer(5, q)[...] = total.astype(bf16)
            remote(buffer(5, q), buffer(4, q), s4.at[p, q.id], v4.at[p, q.id], dev(s_=p)).start()

        if home is None:
            total = summed()
            pl.when(s == p)(functools.partial(keep, total))
            pl.when(s != p)(functools.partial(pass_on, total))
        else:

            @pl.when(s == home)
            def _():
                (keep if home == p else pass_on)(summed())

        if home == p:
            done[q.id, p] = 5
            return
        done[q.id, p] = 4
        plan.add(plan.link(f"x{other(p)}", q.unit, LINK, HOP), functools.partial(r5, q, p))

    def r5(q, p):
        home = q.sum_home(p)

        @pl.when(s == p)
        def _():
            arrived(buffer(4, q), v4.at[p, q.id])
            out = gout(q)
            value = buffer(4, q)[...].astype(f32)
            out[...] = value if home is not None else out[...] + value

        @pl.when(s != p)
        def _():
            arrived(buffer(5, q), s4.at[p, q.id])

        done[q.id, p] = 5

    def settle(q, p):
        home = q.sum_home(p)
        for k, peer in enumerate(c_peers):
            arrived(gwin(q, p, ALL, ALL, peer), s1.at[p, q.id, k])

        def plane():
            for k, peer in enumerate(b_peers):
                arrived(gwin(q, p, ALL, peer, t), s2.at[p, q.id, k])
            for k, peer in enumerate(a_peers):
                arrived(gwin(q, p, peer, b, t), s3.at[p, q.id, k])

        on(home, plane)
        if home is not None:

            @pl.when(s != home)
            def _():
                arrived(gwin(q, p, ALL, ALL, t), r.s6.at[p, q.id])

    def add_into(mine, others):
        lead = mine.shape[:-2]
        count = int(np.prod(lead))

        def one(i, _):
            index = []
            rest = i
            for extent in reversed(lead):
                index.append(lax.rem(rest, extent))
                rest = rest // extent
            index = tuple(reversed(index))
            total = mine[index].astype(f32)
            for o in others:
                total = total + o[index].astype(f32)
            mine[index] = total.astype(bf16)
            return 0

        lax.fori_loop(0, count, one, 0)

    lists = [
        [dev(t_=p) for p in c_peers],
        [dev(b_=p) for p in b_peers],
        [dev(a_=p) for p in a_peers],
    ]
    takes = [r.ra, r.rc, r.rd]
    ss, sv = r.ss, r.sv

    def sum_send(p, k):
        if k == 0:
            r.sums[p, 0] = SG[p].astype(bf16)
        src = r.sums.at[p, k]
        if k < 3:
            for j, target in enumerate(lists[k]):
                send(src, takes[k].at[p, j], ss.at[p, k, j], sv.at[p, k, j], target)
        else:

            @pl.when(s != p)
            def _():
                send(src, r.rb, ss.at[p, k, 0], sv.at[p, k, 0], dev(s_=p))

        size = SG.size * nt * (na if k == 2 else 1)
        link = ("c", "y", "z", f"x{other(p)}")[k]
        when = link_of(link, None, size) if k in (1, 2) else plan.link(link, size, LINK, HOP)
        plan.add(when, functools.partial(sum_take, p, k))

    def sum_take(p, k):
        total = r.sums[p, k].astype(f32)
        if k < 3:
            for j in range(len(lists[k])):
                arrived(takes[k].at[p, j], sv.at[p, k, j])
                total = total + takes[k][p, j].astype(f32)
            r.sums[p, k + 1] = total.astype(bf16)
            sum_send(p, k + 1)
        else:

            @pl.when(s == p)
            def _():
                arrived(r.rb, sv.at[p, k, 0])
                r.small_out[...] = total + r.rb[...].astype(f32)

    def sums_sent():
        for p in range(ns):
            for k in range(3):
                for j in range(len(lists[k])):
                    arrived(r.sums.at[p, k], ss.at[p, k, j])

            @pl.when(s != p)
            def _():
                arrived(r.sums.at[p, 3], ss.at[p, 3, 0])

    def is_sum(step, names):
        return step.func is sum_take and (r3 in names and step.args[1] < 2 or r4 in names)

    first = [q for q in pieces if q.kind == QKV]
    plan.pop()
    for q in first:
        go_z(q, 0)
    plan.until(plan.clock)
    proj = [q for q in pieces if q.kind == PROJ]
    mixed = [q for k in range(2) for q in pieces if q.kind in (FC1, FC2) and q.index == k]
    order = [(q, 0) for q in proj + mixed] + [(q, 1) for q in first + proj + mixed]

    def z_free(q, p):
        return max(plan.free.get(f"z{h}", 0.0) for h in planes(q.home(p)))

    def next_z(k):
        q, p = order[k]
        go_z(q, p)
        if k + 1 < len(order):
            after = order[k + 1]
            plan.add(
                max(x_at[after[0].id, after[1]], z_free(*after) - 8.0), functools.partial(next_z, k + 1)
            )

    plan.add(x_at[order[0][0].id, 0], functools.partial(next_z, 0))
    for q in range(ns):
        arrived(tbl.at[q, t], r.tx.at[q])
        for k, peer in enumerate(c_peers):
            send(tbl.at[q, t], tbl.at[q, t], r.tcs.at[q, k], r.tcr.at[q, k], dev(t_=peer))
    spent(0.5)
    image_ready(0)
    load_rows(0, X)
    spent(0.3)
    for q in range(ns):
        for k, source in enumerate(c_from):
            arrived(tbl.at[q, source], r.tcr.at[q, k])
    for p in range(2):
        build_bias(p)
        spent(0.7)
    image_ready(1)
    load_rows(1, G)
    spent(0.2)

    for p in range(2):
        forward(p)
    for p in (1, 0):
        backward(p)

    for steps_of in ((r1, r2, r2x, r3), (r4,), (r5, sum_take)):
        while plan.pop_of(lambda step: step.func in steps_of or is_sum(step, steps_of)):
            pass

    for q in pieces:
        for p in range(2):
            settle(q, p)
    small_sent()
    received(0)
    received(1)
    shipped(1, 1, 0)
    shipped(1, 0, 1)
    for k in range(ns - 1):
        arrived(r.tbl_in, r.txs.at[k])
    for q in range(ns):
        for k in range(nt - 1):
            arrived(tbl.at[q, t], r.tcs.at[q, k])
    for j, src in enumerate((r.images, r.cotangent)):
        for k in range(nt - 1):
            arrived(outb.at[j, t], r.xcs.at[j, k])
    sums_sent()


def per_device(z, images, cotangent, norm1_gain, norm1_bias, qkv_weight, qkv_bias, position_table,
               proj_weight, proj_bias, norm2_gain, norm2_bias, fc1_weight, fc1_bias, fc2_weight,
               fc2_bias):
    s = lax.axis_index(SECTION)
    d = lax.axis_index(DP)
    t = lax.axis_index(TENSOR)
    D, nt, na, nb, ns, ni = z.d, z.parts, z.na, z.nb, z.sections, z.ni
    part = t * z.dp + d

    def spread_to(values, width, at):
        blank = jnp.zeros((values.shape[0], width), bf16)
        return lax.dynamic_update_slice(blank, values, (0, at))

    vectors = jnp.concatenate(
        [norm1_gain, norm1_bias, proj_bias, norm2_gain, norm2_bias, fc2_bias], 0
    )
    vectors = jnp.where(t == 0, vectors, jnp.zeros_like(vectors))
    small = jnp.concatenate(
        [
            spread_to(vectors, D, d * vectors.shape[1]),
            spread_to(qkv_bias[0], D, part * qkv_bias.shape[-1]),
            spread_to(fc1_bias, z.ff, part * fc1_bias.shape[-1]).reshape(-1, D),
        ],
        0,
    )
    small = jnp.pad(small, ((0, GATHER_ROWS - small.shape[0]), (0, 0)))
    table = jnp.pad(position_table[0].T, ((0, 0), (0, TABLE_PAD - position_table.shape[1])))
    perm = window_permutation(nt, z.half, z.hp)

    qrow, prow, f2row = qkv_weight.shape[1], proj_weight.shape[1], fc2_weight.shape[1]
    m, mw, nch = z.m, z.mw, z.nch
    S = jax.ShapeDtypeStruct
    V = pl.BlockSpec(memory_space=pltpu.VMEM)
    A = pl.BlockSpec(memory_space=pl.ANY)
    dma = pltpu.SemaphoreType.DMA
    reg = pltpu.SemaphoreType.REGULAR
    inputs = dict(
        images=(images, A),
        cotangent=(cotangent, A),
        q_in=(qkv_weight[0].transpose(1, 0, 2), A),
        p_in=(proj_weight[0], A),
        f1_in=(fc1_weight[0], A),
        f2_in=(fc2_weight[0], A),
        sm_in=(small, V),
        tbl_in=(table, V),
        pm=(jnp.asarray(perm, bf16), V),
        pmt=(jnp.asarray(perm.transpose(0, 2, 1), bf16), V),
    )
    wide = D + TABLE_PAD
    outputs = dict(
        act=(S(images.shape, bf16), A),
        ig=(S(images.shape, bf16), A),
        gq_out=(S((3, qrow, D // nt), f32), V),
        gp_out=(S((prow, D), f32), V),
        g1_out=(S((qrow, z.ff // nt), f32), V),
        g2_out=(S((f2row, D), f32), V),
        small_out=(S((GATHER_ROWS, wide), f32), V),
        spill=(S((2, nch, m, CH), bf16), A),
    )
    vm = pltpu.VMEM
    z.pieces = make_pieces(z, qrow, prow, f2row)
    W = len(z.pieces)
    scratch = dict(
        wq=vm((2, 3, nt, na, nb, qrow, D // nt), bf16),
        wp=vm((2, nt, na, nb, prow, D), bf16),
        w1=vm((2, nt, 2, na, nb, qrow, z.ff // nt // 2), bf16),
        w2=vm((2, nt, na, nb, f2row, D), bf16),
        p0=vm((2, GATHER_ROWS, D), bf16),
        p1=vm((2, GATHER_ROWS, D), bf16),
        p2=vm((2, GATHER_ROWS, D), bf16),
        pa=vm((na - 1, 2, GATHER_ROWS, D), bf16),
        pb=vm((nb - 1, 2, GATHER_ROWS, D), bf16),
        pc=vm((nt - 1, 2, GATHER_ROWS, D), bf16),
        ps=dma((4, max(na, nb, nt, ns))),
        psr=dma((4, max(na, nb, nt, ns))),
        ws=dma((W, 2, na)),
        wr=dma((W, 2, na)),
        smf=vm((2, GATHER_ROWS, D), f32),
        tbl=vm((2, nt, z.heads_part, TABLE_PAD), f32),
        outb=vm((2, nt, ni, z.half, D), bf16),
        bm=vm((1 + NW, z.ng, WP, z.quad * WP), f32),
        g=vm((m, D), bf16),
        fn=vm((2, m, D), bf16),
        n1=vm((2, m, D), bf16),
        k=vm((m, 4), f32),
        qk=vm((2, 3, mw, D), bf16),
        pr=vm((2, ni * NW, z.ng, WP, z.quad * WP), bf16),
        ctx=vm((mw, D), bf16),
        ctxt=vm((2, m, D), bf16),
        mid=vm((m, D), f32),
        mg=vm((m, D), f32),
        sn=vm((2, m, D), bf16),
        n2=vm((2, m, D), bf16),
        actv=vm((nch, m, CH), bf16),
        sl=vm((nch, m, CH), bf16),
        sg=vm((2, GATHER_ROWS, wide), f32),
        db=vm((z.ng, WP, z.quad * WP), f32),
        gq=vm((3, nt, na, nb, qrow, D // nt), bf16),
        gp=vm((nt, na, nb, prow, D), bf16),
        g1=vm((nt, 2, na, nb, qrow, z.ff // nt // 2), bf16),
        g2=vm((nt, na, nb, f2row, D), bf16),
        sums=vm((2, 4, GATHER_ROWS, wide), bf16),
        ra=vm((2, nt - 1, GATHER_ROWS, wide), bf16),
        rb=vm((GATHER_ROWS, wide), bf16),
        rc=vm((2, nb - 1, GATHER_ROWS, wide), bf16),
        rd=vm((2, na - 1, GATHER_ROWS, wide), bf16),
        lx=dma((W, ns)),
        xs=dma((W,)),
        zs=dma((W, 2, na - 1)),
        zr=dma((W, 2, na - 1)),
        ys=dma((W, 2, na, nb - 1)),
        yr=dma((W, 2, na, nb - 1)),
        cs=dma((W, 2, na, nt - 1)),
        cr=dma((W, 2, na, nt - 1)),
        tx=dma((ns,)),
        txs=dma((ns - 1,)),
        tcs=dma((ns, nt - 1)),
        tcr=dma((ns, nt - 1)),
        xl=dma((2,)),
        xcs=dma((2, nt - 1)),
        xcr=dma((2, nt - 1)),
        os=dma((2, 2, nt)),
        orr=dma((2, ns * nt)),
        sp=dma((2,)),
        s1=dma((2, W, nt - 1)),
        v1=dma((2, W, nt - 1)),
        s2=dma((2, W, nb - 1)),
        v2=dma((2, W, nb - 1)),
        s3=dma((2, W, na - 1)),
        v3=dma((2, W, na - 1)),
        s4=dma((2, W)),
        v4=dma((2, W)),
        s6=dma((2, W)),
        v6=dma((2, W)),
        k6=reg((W, 1)),
        k1=reg((W, nt - 1)),
        k2=reg((W, nb - 1)),
        k3=reg((W, na - 1)),
        ss=dma((2, 4, max(na, nb, nt, ns))),
        sv=dma((2, 4, max(na, nb, nt, ns))),
    )
    for q in z.pieces:
        scratch[f"r1_{q.id}"] = vm((nt - 1, na, nb, q.rows, q.cols), bf16)
        scratch[f"r2_{q.id}"] = vm((nb - 1, na, q.rows, q.cols), bf16)
        scratch[f"r3_{q.id}"] = vm((na - 1, q.rows, q.cols), bf16)
        scratch[f"r4_{q.id}"] = vm((q.rows, q.cols), bf16)
        scratch[f"r5_{q.id}"] = vm((q.rows, q.cols), bf16)
        if q.sum_home(0) is not None:
            scratch[f"r6_{q.id}"] = vm((na, nb, q.rows, q.cols), bf16)
    z.names = list(inputs) + list(outputs) + list(scratch)
    results = pl.pallas_call(
        functools.partial(kernel, z),
        out_shape=tuple(o for o, _ in outputs.values()),
        in_specs=[spec for _, spec in inputs.values()],
        out_specs=tuple(spec for _, spec in outputs.values()),
        scratch_shapes=list(scratch.values()),
        compiler_params=pltpu.CompilerParams(
            collective_id=0, has_side_effects=True, vmem_limit_bytes=67043328
        ),
        name="two_blocks",
    )(*[x for x, _ in inputs.values()])
    act, ig, gq, gp, g1, g2, sums, _ = results

    def own_vector(k):
        width = norm1_gain.shape[1]
        return lax.dynamic_slice(sums, (k, d * width), (1, width))

    width = qkv_bias.shape[-1]
    qkv_bias_grad = lax.dynamic_slice(sums, (6, part * width), (3, width))[None]
    width = fc1_bias.shape[1]
    fc1_flat = sums[9 : 9 + nch, :D].reshape(1, -1)
    fc1_bias_grad = lax.dynamic_slice(fc1_flat, (0, part * width), (1, width))
    tables = lax.dynamic_slice(sums, (t * z.heads_part, D), (z.heads_part, TABLE_PAD))
    tables = tables[:, : position_table.shape[1]][:, ::-1].T[None]
    return (
        act[None],
        ig[None],
        own_vector(0),
        own_vector(1),
        gq.transpose(1, 0, 2)[None],
        qkv_bias_grad,
        tables,
        gp[None],
        own_vector(2),
        own_vector(3),
        own_vector(4),
        g1[None],
        fc1_bias_grad,
        g2[None],
        own_vector(5),
    )


def solution(mesh):
    def run(*args):
        z = Sizes(mesh, args[0], args[11])
        return per_device(z, *args)

    in_specs = (
        P(DP, TENSOR, None),
        P(DP, TENSOR, None),
        P(SECTION, DP),
        P(SECTION, DP),
        P(SECTION, DP, None, TENSOR),
        P(SECTION, None, (TENSOR, DP)),
        P(SECTION, None, TENSOR),
        P(SECTION, (TENSOR, DP), None),
        P(SECTION, DP),
        P(SECTION, DP),
        P(SECTION, DP),
        P(SECTION, DP, TENSOR),
        P(SECTION, (TENSOR, DP)),
        P(SECTION, (TENSOR, DP), None),
        P(SECTION, DP),
    )
    out_specs = (
        P(SECTION, DP, TENSOR, None),
        P(SECTION, DP, TENSOR, None),
        P(SECTION, DP),
        P(SECTION, DP),
        P(SECTION, DP, None, TENSOR),
        P(SECTION, None, (TENSOR, DP)),
        P(SECTION, None, TENSOR),
        P(SECTION, (TENSOR, DP), None),
        P(SECTION, DP),
        P(SECTION, DP),
        P(SECTION, DP),
        P(SECTION, DP, TENSOR),
        P(SECTION, (TENSOR, DP)),
        P(SECTION, (TENSOR, DP), None),
        P(SECTION, DP),
    )
    return jax.shard_map(
        run, mesh=mesh, in_specs=in_specs, out_specs=out_specs, check_vma=False
    )
```

profile of v0, /device:TPU:0, one launch (start us, length us, event | category | flops | bytes accessed | tf_op | source)
XLA Modules:
  0.0 207.2 jit_solution(13386167509901012020)
XLA Ops:
  0.7 0.8 concatenate.6
  1.4 0.0 copy-start.1
  1.4 0.9 dynamic_update_slice.10
  2.3 1.3 pad.9.refs_7_
  3.7 0.7 constant_dynamic-update-slice_fusion
  4.4 0.2 dynamic_update_slice.9
  4.5 0.6 fusion.4.refs_6_
  5.2 3.5 %copy.32.refs_0_ = bf16[16,98,512]{2,1,0:T(8,128)(2,1)} copy(bf16[16,98,512]{2,0,1:T(8,128)(2,1)} %param.17) | data formatting | bytes 3211264 | tf_op args[0]
  8.7 0.0 copy-done.1
  8.7 2.1 %copy.33.refs_1_ = bf16[16,98,512]{2,1,0:T(8,128)(2,1)} copy(bf16[16,98,512]{2,0,1:T(8,128)(2,1)S(1)} %copy-done.1) | data formatting | bytes 3211264 | tf_op args[1]
  10.8 183.1 %two_blocks.1 = (bf16[16,98,512]{2,1,0:T(8,128)(2,1)}, bf16[16,98,512]{2,1,0:T(8,128)(2,1)}, f32[3,64,256]{2,1,0:T(8,128)}, f32[32,512]{1,0:T(8,128)}, f32[64,10...) custom-call(bf16[16,98,512]{2,1,0:T(8,128)(2,1)} %copy.32.refs_0_, ...), custom_call_target="tpu_custom_call" | custom-call | tf_op jit(solution)/shard_map/two_blocks/pallas_call | solution.py:1446
  193.9 0.0 copy-start
  193.9 3.2 %copy.34 = bf16[1,16,98,512]{3,1,2,0:T(8,128)(2,1)} copy(bf16[1,16,98,512]{3,2,1,0:T(8,128)(2,1)} %bitcast.30) | data formatting | bytes 3211264
  197.2 0.0 copy-done
  197.2 0.0 copy-start.2
  197.2 1.7 copy.35
  198.9 0.8 dynamic-slice_bitcast_fusion
  199.6 0.6 copy.36
  200.2 1.5 constant_dynamic-slice_fusion.2
  201.7 0.7 constant_dynamic-slice_fusion.7
  202.4 0.7 slice_bitcast_fusion
  203.1 0.5 constant_dynamic-slice_fusion
  203.7 0.1 reverse
  203.8 0.7 slice_bitcast_fusion.1
  204.5 0.0 copy-done.4
  204.5 0.7 copy.45
  205.2 0.0 copy-done.5
  205.2 0.6 copy.46
  205.8 0.0 copy-done.3
  205.8 0.7 copy.47
  206.5 0.0 copy-done.2
  206.5 0.7 copy.48
  (10 shorter events, 0.1 us)
Async XLA Ops:
  1.4 7.2 %copy-start.1 = (bf16[16,98,512]{2,0,1:T(8,128)(2,1)S(1)}, bf16[16,98,512]{2,0,1:T(8,128)(2,1)}, u32[]{:S(2)}) copy-start(bf16[16,98,512]{2,0,1:T(8,128)(2,1)} %param.18) | copy-start | bytes 4816900
  193.9 3.3 %copy-start = (bf16[16,98,512]{2,1,0:T(8,128)(2,1)S(1)}, bf16[16,98,512]{2,1,0:T(8,128)(2,1)}, u32[]{:S(2)}) copy-start(bf16[16,98,512]{2,1,0:T(8,128)(2,1)} %get-tuple-element.23) | copy-start | bytes 4816900
  197.2 7.3 %copy-start.4 = (f32[3,64,256]{2,1,0:T(8,128)S(1)}, f32[3,64,256]{2,1,0:T(8,128)}, u32[]{:S(2)}) copy-start(f32[3,64,256]{2,1,0:T(8,128)} %get-tuple-element.25) | copy-start | bytes 589828
  197.2 8.0 %copy-start.5 = (f32[32,512]{1,0:T(8,128)S(1)}, f32[32,512]{1,0:T(8,128)}, u32[]{:S(2)}) copy-start(f32[32,512]{1,0:T(8,128)} %get-tuple-element.26) | copy-start | bytes 196612
  197.2 8.6 %copy-start.3 = (f32[64,1024]{1,0:T(8,128)S(1)}, f32[64,1024]{1,0:T(8,128)}, u32[]{:S(2)}) copy-start(f32[64,1024]{1,0:T(8,128)} %get-tuple-element.27) | copy-start | bytes 786436
  197.2 9.3 %copy-start.2 = (f32[128,512]{1,0:T(8,128)S(1)}, f32[128,512]{1,0:T(8,128)}, u32[]{:S(2)}) copy-start(f32[128,512]{1,0:T(8,128)} %get-tuple-element.28) | copy-start | bytes 786436
where the time goes:
time: 208 us; the launch traced here: 207 us
  Pallas kernels  183 us (88%)
  local copies, waits for them, and re-layouts  22.7 us (11%)
    pallas_call x1, Pallas kernels, per_device(): pl.pallas_call(functools.partial(kernel, z), out_shape=tuple((o for o, _...  183 us
    unnamed x24, local copies, waits for them, and re-layouts  14.7 us

commit v1 on v0

--- a/solution.py
+++ b/solution.py
@@ -20,6 +20,7 @@
 MASK_FILL = -100.0
 ROOT_HALF = 0.7071067811865476
 INV_ROOT_TWO_PI = 0.3989422804014327
+NEG_LOG2_E = -1.4426950408889634
 
 ACROSS = SIDE // WIN
 NW = ACROSS * ACROSS
@@ -126,6 +127,7 @@
 CORE_HOP = 0.8
 MARGIN = 0.3
 SKEW = 0.0
+LEAD = 4.0
 ZLAG = 0.0
 
 
@@ -175,7 +177,7 @@
         self.unit = rows * cols * 2 * z.parts
 
     def home(self, p):
-        if self.kind == PROJ or (self.kind == QKV and self.index == 2):
+        if self.kind == PROJ or (self.kind == QKV and (p == 1 or self.index == 2)):
             return None
         if self.kind == QKV:
             return p if self.index == 0 else 1 - p
@@ -184,7 +186,7 @@
         return p if self.kind == FC1 else 1 - p
 
     def sum_home(self, p):
-        if self.index == 1 and self.kind in (FC1, FC2):
+        if p == 1 and self.index == 1 and self.kind in (FC1, FC2):
             return 0 if self.kind == FC1 else 1
         return None
 
@@ -282,6 +284,11 @@
     def other(home):
         return 1 - home
 
+    crossings = [(q, p) for p in range(ns) for q in pieces if q.home(p) is not None]
+
+    def crossing(q, p):
+        return crossings.index((q, p))
+
     def own_shard(q):
         return shard(q, r.q_in, r.p_in, r.f1_in, r.f2_in)
 
@@ -313,7 +320,7 @@
         def body():
             arrived(here, lx.at[q.id, p])
             for k, peer in enumerate(a_peers):
-                send(here, here, zs.at[q.id, p, k], zr.at[q.id, p, k], dev(a_=peer))
+                send(here, here, zs.at[q.id, p], zr.at[q.id, p, k], dev(a_=peer))
 
         on(home, body)
         plan.add(plan.clock, functools.partial(go_y, q, p, 0))
@@ -332,7 +339,7 @@
             if k:
                 arrived(here, zr.at[q.id, p, k - 1])
             for j, peer in enumerate(b_peers):
-                send(here, here, ys.at[q.id, p, k, j], yr.at[q.id, p, k, j], dev(b_=peer))
+                send(here, here, ys.at[q.id, p], yr.at[q.id, p, k, j], dev(b_=peer))
 
         on(home, body)
         for j in range(nb - 1):
@@ -342,7 +349,7 @@
     def to_core(q, p, k):
         here = win(q, wref[q.kind], (p,), source_row(k), ALL, t)
         for j, peer in enumerate(c_peers):
-            send(here, here, cs.at[q.id, p, k, j], cr.at[q.id, p, k, j], dev(t_=peer))
+            send(here, here, cs.at[q.id, p, j], cr.at[q.id, p, j], dev(t_=peer))
 
     def core_time(q, p):
         when = plan.link("c", q.unit * nb / nt, CORE_LINK, CORE_HOP)
@@ -357,7 +364,7 @@
                 arrived(win(q, wref[q.kind], (p,), source_row(k), source, t), yr.at[q.id, p, k, j])
             if home is not None:
                 here = win(q, wref[q.kind], (p,), source_row(k), ALL, t)
-                send(here, here, r.ws.at[q.id, p, k], r.wr.at[q.id, p, k], dev(s_=other(home)))
+                send(here, here, r.ws.at[crossing(q, p)], r.wr.at[crossing(q, p), k], dev(s_=other(home)))
             to_core(q, p, k)
 
         on(home, body)
@@ -368,7 +375,7 @@
 
     def go_w(q, p, k):
         def body():
-            arrived(win(q, wref[q.kind], (p,), source_row(k), ALL, t), r.wr.at[q.id, p, k])
+            arrived(win(q, wref[q.kind], (p,), source_row(k), ALL, t), r.wr.at[crossing(q, p), k])
             to_core(q, p, k)
 
         on(other(q.home(p)), body)
@@ -387,16 +394,13 @@
             plan.pop()
         for q in mine:
             plan.clock = max(plan.clock, ready_at[q.id, p])
-            for k in range(na):
-                for j, source in enumerate(c_from):
-                    arrived(win(q, wref[q.kind], (p,), source_row(k), ALL, source), cr.at[q.id, p, k, j])
+            for j, source in enumerate(c_from):
+                arrived(win(q, wref[q.kind], (p,), ALL, ALL, source), cr.at[q.id, p, j])
 
     def gather_sent():
         for q in pieces:
             for p in range(ns):
                 home = q.home(p)
-                here = win(q, wref[q.kind], (p,), a, b, t)
-
                 if home != p:
 
                     @pl.when(s == p)
@@ -404,18 +408,15 @@
                         arrived(own_shard(q), xs.at[q.id])
 
                 def plane():
-                    for k in range(na - 1):
-                        arrived(here, zs.at[q.id, p, k])
-                    for k in range(na):
-                        for j in range(nb - 1):
-                            arrived(here, ys.at[q.id, p, k, j])
-                        if home is not None:
-                            arrived(win(q, wref[q.kind], (p,), a, ALL, t), r.ws.at[q.id, p, k])
+                    ref = wref[q.kind]
+                    arrived(win(q, ref, (p,), pl.ds(0, na - 1), b, t), zs.at[q.id, p])
+                    arrived(win(q, ref, (p,), ALL, pl.ds(0, nb - 1), t), ys.at[q.id, p])
+                    if home is not None:
+                        arrived(win(q, ref, (p,), ALL, ALL, t), r.ws.at[crossing(q, p)])
 
                 on(home, plane)
-                for k in range(na):
-                    for j in range(nt - 1):
-                        arrived(win(q, wref[q.kind], (p,), a, ALL, t), cs.at[q.id, p, k, j])
+                for j in range(nt - 1):
+                    arrived(win(q, wref[q.kind], (p,), ALL, ALL, t), cs.at[q.id, p, j])
 
     def run(lo, hi, cost, body, before=None):
         def one(i, carry):
@@ -443,59 +444,90 @@
     P0, P1, P2 = r.p0, r.p1, r.p2
     small_ready = []
 
+    def placed(ref, at):
+        value = ref[...] if len(ref.shape) == 2 else ref[0]
+        width = value.shape[-1]
+        col = lax.broadcasted_iota(jnp.int32, (width, z.d), 1)
+        src = lax.broadcasted_iota(jnp.int32, (width, z.d), 0)
+        return dotf(value, (col == src + at).astype(bf16), NN)
+
+    def pack_small():
+        share = t * z.dp + d
+        first = (t == 0).astype(f32)
+        index = lax.broadcasted_iota(jnp.int32, (GATHER_ROWS, z.d), 0)
+        total = jnp.zeros((GATHER_ROWS, z.d), f32)
+        vectors = (r.v_n1g, r.v_n1b, r.v_pb, r.v_n2g, r.v_n2b, r.v_f2b)
+        width = r.v_n1g.shape[-1]
+        for k, ref in enumerate(vectors):
+            total = total + jnp.where(index == k, placed(ref, d * width) * first, 0.0)
+        qkv_rows = placed(r.v_qb, share * r.v_qb.shape[-1])
+        for k in range(3):
+            total = total + jnp.where(index == 6 + k, qkv_rows[k : k + 1], 0.0)
+        at = share * r.v_f1b.shape[-1]
+        total = total + jnp.where(index == 9 + at // z.d, placed(r.v_f1b, lax.rem(at, z.d)), 0.0)
+        r.sm_in[...] = total.astype(bf16)
+
     def small_start():
         P0[s] = r.sm_in[...]
         for k, peer in enumerate(x_peers):
-            send(r.sm_in, P0.at[s], r.ps.at[0, k], r.psr.at[0, k], dev(s_=peer))
-        plan.add(plan.link("x0", P0.size * nt, LINK, HOP), small_a)
-
-    def small_part(src, dst, level, targets):
+            send(r.sm_in, P0.at[s], r.ps.at[0, 0], r.psr.at[0, 0], dev(s_=peer))
+        plan.link("x0", P0.size * nt, LINK, HOP)
+
+    def small_part(src, dst, p, level, targets):
         for k, target in enumerate(targets):
-            send(src, dst.at[k], r.ps.at[level, k], r.psr.at[level, k], target)
-
-    def small_sum(base, takes, level):
-        total = base[...].astype(f32)
-        for k in range(takes.shape[0]):
-            arrived(takes.at[k], r.psr.at[level, k])
-            total = total + takes[k].astype(f32)
+            send(src.at[p], dst.at[p, k], r.ps.at[p, level], r.psr.at[p, level], target)
+
+    def small_sum(base, takes, p, level):
+        total = base[p].astype(f32)
+        arrived(takes.at[p], r.psr.at[p, level])
+        for k in range(takes.shape[1]):
+            total = total + takes[p, k].astype(f32)
         return total
 
-    def small_a():
-        for k, source in enumerate(x_from):
-            arrived(P0.at[source], r.psr.at[0, k])
-        small_part(P0, r.pa, 1, [dev(a_=p) for p in a_peers])
+    def small_a(p):
+        @pl.when(s != p)
+        def _():
+            arrived(P0.at[p], r.psr.at[0, 0])
+
+        small_part(P0, r.pa, p, 1, [dev(a_=e) for e in a_peers])
         for h in range(ns):
-            when = plan.link(f"z{h}", P0.size * 2 * nt * na + SKEW * LINK, LINK, HOP)
-        plan.add(when, small_b)
-
-    def small_b():
-        P1[...] = small_sum(P0, r.pa, 1).astype(bf16)
-        small_part(P1, r.pb, 2, [dev(b_=p) for p in b_peers])
-        plan.add(plan.link("y0", P0.size * 2 * nt, LINK, HOP), small_c)
-
-    def small_c():
-        P2[...] = small_sum(P1, r.pb, 2).astype(bf16)
-        small_part(P2, r.pc, 3, [dev(t_=p) for p in c_peers])
-        plan.add(plan.clock + CORE_HOP, small_d)
-
-    def small_d():
-        SMF[...] = small_sum(P2, r.pc, 3)
-        small_ready.append(True)
-
-    def need_small():
-        while not small_ready:
+            when = plan.link(f"z{h}", P0.size * nt * na, LINK, HOP)
+        plan.add(when, functools.partial(small_b, p))
+
+    def small_b(p):
+        P1[p] = small_sum(P0, r.pa, p, 1).astype(bf16)
+        small_part(P1, r.pb, p, 2, [dev(b_=e) for e in b_peers])
+        for h in range(ns):
+            when = plan.link(f"y{h}", P0.size * nt, LINK, HOP)
+        plan.add(when, functools.partial(small_c, p))
+
+    def small_c(p):
+        P2[p] = small_sum(P1, r.pb, p, 2).astype(bf16)
+        small_part(P2, r.pc, p, 3, [dev(t_=e) for e in c_peers])
+        plan.add(plan.clock + CORE_HOP, functools.partial(small_d, p))
+
+    def small_d(p):
+        SMF[p] = small_sum(P2, r.pc, p, 3)
+        small_ready.append(p)
+
+    def need_small(p):
+        while p not in small_ready:
             plan.pop()
 
     def small_sent():
         arrived(r.sm_in, r.ps.at[0, 0])
-        for level, takes in ((1, r.pa), (2, r.pb), (3, r.pc)):
-            for k in range(takes.shape[0]):
-                arrived(takes.at[k], r.ps.at[level, k])
+        for p in range(ns):
+            for level, takes in ((1, r.pa), (2, r.pb), (3, r.pc)):
+                arrived(takes.at[p], r.ps.at[p, level])
 
     group = s * nt + t
 
     def group_images(g):
         return pl.ds(g * ni, ni)
+
+    pack_small()
+    r.tbl_in[...] = jnp.zeros(r.tbl_in.shape, f32)
+    r.tbl_in[:, 0 : r.v_tab.shape[-1]] = r.v_tab[...]
 
     barrier = pltpu.get_barrier_semaphore()
     peers = (
@@ -518,10 +550,10 @@
         start_x(q)
     xin = r.outb
     for j, src in enumerate((r.images, r.cotangent)):
-        pltpu.make_async_copy(src.at[group_images(group)], xin.at[j, t], r.xl.at[j]).start()
+        pltpu.make_async_copy(src.at[group_images(t)], xin.at[j, t], r.xl.at[j]).start()
         for k, peer in enumerate(c_peers):
             send(
-                src.at[group_images(s * nt + peer)],
+                src.at[group_images(peer)],
                 xin.at[j, t],
                 r.xcs.at[j, k],
                 r.xcr.at[j, k],
@@ -687,7 +719,7 @@
     SG, DB = r.sg, r.db
 
     def forward(p):
-        need_small()
+        need_small(p)
 
         def ln1(i):
             n, inv = normalize(X[block(i, rows), :])
@@ -724,7 +756,7 @@
             for v, (S, L) in zip(mixed, at):
                 CTX[S, L] = collect(v, mf).astype(bf16)
 
-        run(0, ni * NW // BATCH, 0.72, attention)
+        run(0, ni * NW // BATCH, 0.7, attention)
 
         def unperm(i):
             CTXT[p, block(i, rows), :] = dotf(PMT[p], CTX[block(i, NW * WP), :], NN).astype(bf16)
@@ -754,9 +786,10 @@
             def rise(i):
                 c = j + 2 * i
                 u = dotf(SN[p], w_fc1(p, c), NN) + row(p, 9 + c)
-                e = 0.5 * (1.0 + lax.erf(u * ROOT_HALF))
+                h = u * ROOT_HALF
+                e = 0.5 + 0.5 * lax.erf(h)
                 ACT[c] = (u * e).astype(bf16)
-                SL[c] = (e + u * jnp.exp(-0.5 * u * u) * INV_ROOT_TWO_PI).astype(bf16)
+                SL[c] = (e + (u * INV_ROOT_TWO_PI) * jnp.exp2(h * h * NEG_LOG2_E)).astype(bf16)
 
             run(0, per, 1.16, rise)
         need(FC2, p)
@@ -774,7 +807,7 @@
             X[block(i, rows), :] = value.astype(bf16).astype(f32)
             stage_out(value, i, p)
 
-        run(0, ni, 0.05, finish)
+        run(0, ni, 0.08, finish)
         ship_later(0, p, p, (9.0, 14.0, 19.0, 24.0) if p == 0 else (0.0, 5.0, 10.0, 15.0))
 
     g1_own = r.g1.reshape(z.nch, *w1_all.shape[2:])
@@ -797,7 +830,7 @@
         def fc2_grad(c):
             g2[c] = dotf(ACT[c], G[...], TN).astype(bf16).reshape(g2.shape[1:])
 
-        run(0, z.nch, 0.62, fc2_grad)
+        run(0, z.nch, 0.82, fc2_grad)
         emit(FC2, p)
 
         def hidden(c):
@@ -805,19 +838,19 @@
             SG[p, pl.ds(9 + c, 1), 0 : z.d] = column_sum(hg)
             SL[c] = hg.astype(bf16)
 
-        run(0, z.nch, 0.65, hidden)
+        run(0, z.nch, 0.76, hidden)
 
         def fc1(c):
             g1[c] = dotf(SN[p], SL[c], TN).astype(bf16).reshape(g1.shape[1:])
 
-        run(0, z.nch, 0.75, fc1)
+        run(0, z.nch, 0.85, fc1)
         MID[...] = jnp.zeros(MID.shape, f32)
         emit(FC1, p)
 
         def n2g(c):
             MID[...] += dotf(SL[c], w_fc1(p, c), NT)
 
-        run(0, z.nch, 0.65, n2g)
+        run(0, z.nch, 0.74, n2g)
         if p == 1:
             for j, ref in enumerate((ACT, SL)):
                 pltpu.make_async_copy(r.spill.at[j], ref, r.sp.at[j]).start()
@@ -835,7 +868,7 @@
             addrow(2, column_sum(mg))
             G[sl, :] = mg.astype(bf16)
 
-        run(0, ni, 0.31, ln2)
+        run(0, ni, 0.4, ln2)
         gp[...] = dotf(CTXT[p], G[...], TN).astype(bf16).reshape(gp.shape)
         CTXT[p] = dotf(G[...], w_proj(p), NT).astype(bf16)
         spent(1.2)
@@ -898,7 +931,7 @@
 
         shipped(0, 1 - p, 1 - p)
         per = NW // BATCH
-        cost = 1.6
+        cost = 1.7
 
         def image_step(k):
             attention(k)
@@ -915,7 +948,7 @@
         else:
             ship_later(1, p, 1 - p, [first * ni + 4.0 + 5.0 * i for i in range(ni)])
         run(0, ni * per, cost, image_step)
-        run(0, 3, 0.75, qkv_grad, emit_last)
+        run(0, 3, 0.82, qkv_grad, emit_last)
         emit(QKV, p, 2)
         table_rows(p)
         sum_send(p, 0)
@@ -952,7 +985,7 @@
                 v = pltpu.roll(v, 0, 1, stride=TABLE_SIDE - WIN, stride_axis=0)
                 SG[p, pl.ds(g * z.quad + h, 1), z.d :] = column_sum(v)
 
-        run(0, z.ng, 0.4, one_group)
+        run(0, z.ng, 0.61, one_group)
 
     gref = {QKV: r.gq, PROJ: r.gp, FC1: r.g1, FC2: r.g2}
     s1, v1, s2, v2, s3, v3, s4, v4 = (r.s1, r.v1, r.s2, r.v2, r.s3, r.v3, r.s4, r.v4)
@@ -968,7 +1001,12 @@
         return win(q, gref[q.kind], (), a_, b_, t_)
 
     def gout(q):
-        return shard(q, r.gq_out, r.gp_out, r.g1_out, r.g2_out)
+        return shard(q, r.gq_sum, r.gp_sum, r.g1_sum, r.g2_sum)
+
+    def final(q):
+        return pltpu.make_async_copy(
+            gout(q), shard(q, r.gq_out, r.gp_out, r.g1_out, r.g2_out), r.og.at[q.id]
+        )
 
     def reached(q, p, level):
         while done.get((q.id, p), 0) < level:
@@ -1015,8 +1053,7 @@
 
         @pl.when(s != home)
         def _():
-            spend(r.k6, q, 0, p)
-            send(mine, buffer(6, q), r.s6.at[p, q.id], r.v6.at[p, q.id], dev(s_=home))
+            send(mine, buffer(6, q), r.s6.at[q.id], r.v6.at[q.id], dev(s_=home))
 
         when = plan.link(f"x{other(home)}", q.unit * na * nb, LINK, HOP)
         plan.add(when, functools.partial(r2x, q, p))
@@ -1025,9 +1062,8 @@
         home = q.sum_home(p)
 
         def body():
-            arrived(buffer(6, q), r.v6.at[p, q.id])
+            arrived(buffer(6, q), r.v6.at[q.id])
             add_into(gwin(q, p, ALL, ALL, t), [buffer(6, q)])
-            credit(r.k6, q, 0, p, dev(s_=other(home)))
 
         on(home, body)
         plan.clock += q.unit * na * nb / 10e6
@@ -1038,7 +1074,7 @@
 
         def body():
             for k, peer in enumerate(b_peers):
-                spend(k2, q, k, p)
+                on(q.sum_home(1), functools.partial(spend, k2, q, k, p))
                 send(
                     gwin(q, p, ALL, peer, t),
                     buffer(2, q).at[k],
@@ -1063,13 +1099,14 @@
             add_into(gwin(q, p, ALL, b, t), [buffer(2, q).at[k] for k in range(nb - 1)])
             for k, source in enumerate(b_from):
                 credit(k2, q, k, p, dev(b_=source))
+            if p == 0:
+                on(q.sum_home(1), lambda: pl.semaphore_wait(k3.at[q.id], na - 1))
             for k, peer in enumerate(a_peers):
-                spend(k3, q, k, p)
                 send(
                     gwin(q, p, peer, b, t),
                     buffer(3, q).at[k],
-                    s3.at[p, q.id, k],
-                    v3.at[p, q.id, k],
+                    s3.at[p, q.id],
+                    v3.at[p, q.id],
                     dev(a_=peer),
                 )
 
@@ -1086,13 +1123,15 @@
         mine = gwin(q, p, a, b, t)
 
         def summed():
-            for k in range(na - 1):
-                arrived(buffer(3, q).at[k], v3.at[p, q.id, k])
+            arrived(buffer(3, q), v3.at[p, q.id])
             total = mine[...].astype(f32)
             for k in range(na - 1):
                 total = total + buffer(3, q)[k].astype(f32)
             for k, source in enumerate(a_from):
-                credit(k3, q, k, p, dev(a_=source))
+                if p == 1:
+                    pl.semaphore_signal(
+                        k3.at[q.id], inc=1, device_id=dev(a_=source), device_id_type=MESH
+                    )
             return total
 
         def keep(total):
@@ -1111,6 +1150,8 @@
             @pl.when(s == home)
             def _():
                 (keep if home == p else pass_on)(summed())
+                if home == p:
+                    final(q).start()
 
         if home == p:
             done[q.id, p] = 5
@@ -1127,6 +1168,7 @@
             out = gout(q)
             value = buffer(4, q)[...].astype(f32)
             out[...] = value if home is not None else out[...] + value
+            final(q).start()
 
         @pl.when(s != p)
         def _():
@@ -1142,15 +1184,14 @@
         def plane():
             for k, peer in enumerate(b_peers):
                 arrived(gwin(q, p, ALL, peer, t), s2.at[p, q.id, k])
-            for k, peer in enumerate(a_peers):
-                arrived(gwin(q, p, peer, b, t), s3.at[p, q.id, k])
+            arrived(gwin(q, p, pl.ds(0, na - 1), b, t), s3.at[p, q.id])
 
         on(home, plane)
         if home is not None:
 
             @pl.when(s != home)
             def _():
-                arrived(gwin(q, p, ALL, ALL, t), r.s6.at[p, q.id])
+                arrived(gwin(q, p, ALL, ALL, t), r.s6.at[q.id])
 
     def add_into(mine, others):
         lead = mine.shape[:-2]
@@ -1185,23 +1226,26 @@
         src = r.sums.at[p, k]
         if k < 3:
             for j, target in enumerate(lists[k]):
-                send(src, takes[k].at[p, j], ss.at[p, k, j], sv.at[p, k, j], target)
+                send(src, takes[k].at[p, j], ss.at[p, k], sv.at[p, k], target)
         else:
 
             @pl.when(s != p)
             def _():
-                send(src, r.rb, ss.at[p, k, 0], sv.at[p, k, 0], dev(s_=p))
+                send(src, r.rb, ss.at[p, k], sv.at[p, k], dev(s_=p))
 
         size = SG.size * nt * (na if k == 2 else 1)
         link = ("c", "y", "z", f"x{other(p)}")[k]
         when = link_of(link, None, size) if k in (1, 2) else plan.link(link, size, LINK, HOP)
         plan.add(when, functools.partial(sum_take, p, k))
 
+    def small_final():
+        return pltpu.make_async_copy(r.small_sum, r.small_out, r.og.at[len(pieces)])
+
     def sum_take(p, k):
         total = r.sums[p, k].astype(f32)
         if k < 3:
+            arrived(takes[k].at[p], sv.at[p, k])
             for j in range(len(lists[k])):
-                arrived(takes[k].at[p, j], sv.at[p, k, j])
                 total = total + takes[k][p, j].astype(f32)
             r.sums[p, k + 1] = total.astype(bf16)
             sum_send(p, k + 1)
@@ -1209,26 +1253,27 @@
 
             @pl.when(s == p)
             def _():
-                arrived(r.rb, sv.at[p, k, 0])
-                r.small_out[...] = total + r.rb[...].astype(f32)
+                arrived(r.rb, sv.at[p, k])
+                r.small_sum[...] = total + r.rb[...].astype(f32)
+                small_final().start()
 
     def sums_sent():
         for p in range(ns):
             for k in range(3):
-                for j in range(len(lists[k])):
-                    arrived(r.sums.at[p, k], ss.at[p, k, j])
+                arrived(takes[k].at[p], ss.at[p, k])
 
             @pl.when(s != p)
             def _():
-                arrived(r.sums.at[p, 3], ss.at[p, 3, 0])
+                arrived(r.sums.at[p, 3], ss.at[p, 3])
 
     def is_sum(step, names):
         return step.func is sum_take and (r3 in names and step.args[1] < 2 or r4 in names)
 
     first = [q for q in pieces if q.kind == QKV]
-    plan.pop()
     for q in first:
         go_z(q, 0)
+    small_a(0)
+    plan.add(plan.clock + 18.0, functools.partial(small_a, 1))
     plan.until(plan.clock)
     proj = [q for q in pieces if q.kind == PROJ]
     mixed = [q for k in range(2) for q in pieces if q.kind in (FC1, FC2) and q.index == k]
@@ -1243,7 +1288,7 @@
         if k + 1 < len(order):
             after = order[k + 1]
             plan.add(
-                max(x_at[after[0].id, after[1]], z_free(*after) - 8.0), functools.partial(next_z, k + 1)
+                max(x_at[after[0].id, after[1]], z_free(*after) - LEAD), functools.partial(next_z, k + 1)
             )
 
     plan.add(x_at[order[0][0].id, 0], functools.partial(next_z, 0))
@@ -1277,6 +1322,9 @@
     for q in pieces:
         for p in range(2):
             settle(q, p)
+    for q in pieces:
+        final(q).wait()
+    small_final().wait()
     small_sent()
     received(0)
     received(1)
@@ -1302,24 +1350,9 @@
     D, nt, na, nb, ns, ni = z.d, z.parts, z.na, z.nb, z.sections, z.ni
     part = t * z.dp + d
 
-    def spread_to(values, width, at):
-        blank = jnp.zeros((values.shape[0], width), bf16)
-        return lax.dynamic_update_slice(blank, values, (0, at))
-
-    vectors = jnp.concatenate(
-        [norm1_gain, norm1_bias, proj_bias, norm2_gain, norm2_bias, fc2_bias], 0
-    )
-    vectors = jnp.where(t == 0, vectors, jnp.zeros_like(vectors))
-    small = jnp.concatenate(
-        [
-            spread_to(vectors, D, d * vectors.shape[1]),
-            spread_to(qkv_bias[0], D, part * qkv_bias.shape[-1]),
-            spread_to(fc1_bias, z.ff, part * fc1_bias.shape[-1]).reshape(-1, D),
-        ],
-        0,
-    )
-    small = jnp.pad(small, ((0, GATHER_ROWS - small.shape[0]), (0, 0)))
-    table = jnp.pad(position_table[0].T, ((0, 0), (0, TABLE_PAD - position_table.shape[1])))
+    def chosen(values):
+        return lax.dynamic_slice_in_dim(values, s * nt * ni, nt * ni, 0)
+
     perm = window_permutation(nt, z.half, z.hp)
 
     qrow, prow, f2row = qkv_weight.shape[1], proj_weight.shape[1], fc2_weight.shape[1]
@@ -1330,14 +1363,21 @@
     dma = pltpu.SemaphoreType.DMA
     reg = pltpu.SemaphoreType.REGULAR
     inputs = dict(
-        images=(images, A),
-        cotangent=(cotangent, A),
+        images=(chosen(images), A),
+        cotangent=(chosen(cotangent), A),
         q_in=(qkv_weight[0].transpose(1, 0, 2), A),
         p_in=(proj_weight[0], A),
         f1_in=(fc1_weight[0], A),
         f2_in=(fc2_weight[0], A),
-        sm_in=(small, V),
-        tbl_in=(table, V),
+        v_n1g=(norm1_gain, V),
+        v_n1b=(norm1_bias, V),
+        v_pb=(proj_bias, V),
+        v_n2g=(norm2_gain, V),
+        v_n2b=(norm2_bias, V),
+        v_f2b=(fc2_bias, V),
+        v_qb=(qkv_bias[0], V),
+        v_f1b=(fc1_bias, V),
+        v_tab=(position_table[0].T, V),
         pm=(jnp.asarray(perm, bf16), V),
         pmt=(jnp.asarray(perm.transpose(0, 2, 1), bf16), V),
     )
@@ -1345,31 +1385,40 @@
     outputs = dict(
         act=(S(images.shape, bf16), A),
         ig=(S(images.shape, bf16), A),
-        gq_out=(S((3, qrow, D // nt), f32), V),
-        gp_out=(S((prow, D), f32), V),
-        g1_out=(S((qrow, z.ff // nt), f32), V),
-        g2_out=(S((f2row, D), f32), V),
-        small_out=(S((GATHER_ROWS, wide), f32), V),
+        gq_out=(S((3, qrow, D // nt), f32), A),
+        gp_out=(S((prow, D), f32), A),
+        g1_out=(S((qrow, z.ff // nt), f32), A),
+        g2_out=(S((f2row, D), f32), A),
+        small_out=(S((GATHER_ROWS, wide), f32), A),
         spill=(S((2, nch, m, CH), bf16), A),
     )
     vm = pltpu.VMEM
     z.pieces = make_pieces(z, qrow, prow, f2row)
     W = len(z.pieces)
+    cross = sum(q.home(p) is not None for q in z.pieces for p in range(2))
     scratch = dict(
         wq=vm((2, 3, nt, na, nb, qrow, D // nt), bf16),
         wp=vm((2, nt, na, nb, prow, D), bf16),
         w1=vm((2, nt, 2, na, nb, qrow, z.ff // nt // 2), bf16),
         w2=vm((2, nt, na, nb, f2row, D), bf16),
+        gq_sum=vm((3, qrow, D // nt), f32),
+        gp_sum=vm((prow, D), f32),
+        g1_sum=vm((qrow, z.ff // nt), f32),
+        g2_sum=vm((f2row, D), f32),
+        small_sum=vm((GATHER_ROWS, wide), f32),
+        og=dma((W + 1,)),
+        sm_in=vm((GATHER_ROWS, D), bf16),
+        tbl_in=vm((z.heads_part, TABLE_PAD), f32),
         p0=vm((2, GATHER_ROWS, D), bf16),
         p1=vm((2, GATHER_ROWS, D), bf16),
         p2=vm((2, GATHER_ROWS, D), bf16),
-        pa=vm((na - 1, 2, GATHER_ROWS, D), bf16),
-        pb=vm((nb - 1, 2, GATHER_ROWS, D), bf16),
-        pc=vm((nt - 1, 2, GATHER_ROWS, D), bf16),
-        ps=dma((4, max(na, nb, nt, ns))),
-        psr=dma((4, max(na, nb, nt, ns))),
-        ws=dma((W, 2, na)),
-        wr=dma((W, 2, na)),
+        pa=vm((2, na - 1, GATHER_ROWS, D), bf16),
+        pb=vm((2, nb - 1, GATHER_ROWS, D), bf16),
+        pc=vm((2, nt - 1, GATHER_ROWS, D), bf16),
+        ps=dma((2, 4)),
+        psr=dma((2, 4)),
+        ws=dma((cross,)),
+        wr=dma((cross, na)),
         smf=vm((2, GATHER_ROWS, D), f32),
         tbl=vm((2, nt, z.heads_part, TABLE_PAD), f32),
         outb=vm((2, nt, ni, z.half, D), bf16),
@@ -1401,12 +1450,12 @@
         rd=vm((2, na - 1, GATHER_ROWS, wide), bf16),
         lx=dma((W, ns)),
         xs=dma((W,)),
-        zs=dma((W, 2, na - 1)),
+        zs=dma((W, 2)),
         zr=dma((W, 2, na - 1)),
-        ys=dma((W, 2, na, nb - 1)),
+        ys=dma((W, 2)),
         yr=dma((W, 2, na, nb - 1)),
-        cs=dma((W, 2, na, nt - 1)),
-        cr=dma((W, 2, na, nt - 1)),
+        cs=dma((W, 2, nt - 1)),
+        cr=dma((W, 2, nt - 1)),
         tx=dma((ns,)),
         txs=dma((ns - 1,)),
         tcs=dma((ns, nt - 1)),
@@ -1421,18 +1470,17 @@
         v1=dma((2, W, nt - 1)),
         s2=dma((2, W, nb - 1)),
         v2=dma((2, W, nb - 1)),
-        s3=dma((2, W, na - 1)),
-        v3=dma((2, W, na - 1)),
+        s3=dma((2, W)),
+        v3=dma((2, W)),
         s4=dma((2, W)),
         v4=dma((2, W)),
-        s6=dma((2, W)),
-        v6=dma((2, W)),
-        k6=reg((W, 1)),
+        s6=dma((W,)),
+        v6=dma((W,)),
         k1=reg((W, nt - 1)),
         k2=reg((W, nb - 1)),
-        k3=reg((W, na - 1)),
-        ss=dma((2, 4, max(na, nb, nt, ns))),
-        sv=dma((2, 4, max(na, nb, nt, ns))),
+        k3=reg((W,)),
+        ss=dma((2, 4)),
+        sv=dma((2, 4)),
     )
     for q in z.pieces:
         scratch[f"r1_{q.id}"] = vm((nt - 1, na, nb, q.rows, q.cols), bf16)
@@ -1440,7 +1488,7 @@
         scratch[f"r3_{q.id}"] = vm((na - 1, q.rows, q.cols), bf16)
         scratch[f"r4_{q.id}"] = vm((q.rows, q.cols), bf16)
         scratch[f"r5_{q.id}"] = vm((q.rows, q.cols), bf16)
-        if q.sum_home(0) is not None:
+        if q.sum_home(1) is not None:
             scratch[f"r6_{q.id}"] = vm((na, nb, q.rows, q.cols), bf16)
     z.names = list(inputs) + list(outputs) + list(scratch)
     results = pl.pallas_call(

time: 208 us -> 194 us (0.933)
  Pallas kernels: 183 us -> 176 us
  local copies, waits for them, and re-layouts: 22.7 us -> 17 us
    pallas_call x1, Pallas kernels: 183 us -> 176 us  [per_device(): pl.pallas_call(functools.partial(kernel, z), out_shape=tuple((o for o, _...]
    unnamed x24 -> x22, local copies, waits for them, and re-layouts: 14.7 us -> 11.4 us
where the time goes in v1:
time: 194 us
  Pallas kernels  176 us (91%)
  local copies, waits for them, and re-layouts  17 us (9%)
    pallas_call x1, Pallas kernels, per_device(): pl.pallas_call(functools.partial(kernel, z), out_shape=tuple((o for o, _...  176 us
    unnamed x22, local copies, waits for them, and re-layouts  11.4 us

profile of v1, /device:TPU:0, one launch (start us, length us, event | category | flops | bytes accessed | tf_op | source)
XLA Modules:
  0.0 193.6 jit_solution(874807431742019972)
XLA Ops:
  0.7 1.5 constant_dynamic-slice_fusion.2
  2.1 1.1 copy.37.refs_0_
  3.3 1.1 copy.38.refs_1_
  4.4 175.9 %two_blocks.1 = (bf16[16,98,512]{2,1,0:T(8,128)(2,1)}, bf16[16,98,512]{2,1,0:T(8,128)(2,1)}, f32[3,64,256]{2,1,0:T(8,128)}, f32[32,512]{1,0:T(8,128)}, f32[64,10...) custom-call(bf16[8,98,512]{2,1,0:T(8,128)(2,1)} %copy.37.refs_0_, ...), custom_call_target="tpu_custom_call" | custom-call | tf_op jit(solution)/shard_map/two_blocks/pallas_call | solution.py:1494
  180.3 0.7 slice_bitcast_fusion
  181.1 0.5 constant_dynamic-slice_fusion
  181.6 0.8 dynamic-slice_bitcast_fusion
  182.3 0.6 copy.36
  182.9 1.5 constant_dynamic-slice_fusion.4
  184.4 0.7 constant_dynamic-slice_fusion.8
  185.1 0.1 reverse
  185.3 0.7 slice_bitcast_fusion.1
  185.9 0.0 copy-start
  185.9 3.2 %copy.34 = bf16[1,16,98,512]{3,1,2,0:T(8,128)(2,1)} copy(bf16[1,16,98,512]{3,2,1,0:T(8,128)(2,1)} %bitcast.30) | data formatting | bytes 3211264
  189.2 0.0 copy-done
  189.2 0.0 copy-start.3
  189.2 0.0 copy-start.4
  189.2 0.0 copy-start.2
  189.2 0.0 copy-start.1
  189.2 1.7 copy.35
  190.9 0.0 copy-done.3
  190.9 0.7 copy.44
  191.5 0.0 copy-done.4
  191.5 0.6 copy.45
  192.2 0.0 copy-done.2
  192.2 0.7 copy.46
  192.9 0.0 copy-done.1
  192.9 0.7 copy.47
  (1 shorter events, 0.0 us)
Async XLA Ops:
  185.9 3.2 %copy-start = (bf16[16,98,512]{2,1,0:T(8,128)(2,1)S(1)}, bf16[16,98,512]{2,1,0:T(8,128)(2,1)}, u32[]{:S(2)}) copy-start(bf16[16,98,512]{2,1,0:T(8,128)(2,1)} %get-tuple-element.23) | copy-start | bytes 4816900
  189.2 1.7 copy-start.3
  189.2 2.4 %copy-start.4 = (f32[32,512]{1,0:T(8,128)S(1)}, f32[32,512]{1,0:T(8,128)}, u32[]{:S(2)}) copy-start(f32[32,512]{1,0:T(8,128)} %get-tuple-element.26) | copy-start | bytes 196612
  189.2 3.0 %copy-start.2 = (f32[64,1024]{1,0:T(8,128)S(1)}, f32[64,1024]{1,0:T(8,128)}, u32[]{:S(2)}) copy-start(f32[64,1024]{1,0:T(8,128)} %get-tuple-element.27) | copy-start | bytes 786436
  189.2 3.7 %copy-start.1 = (f32[128,512]{1,0:T(8,128)S(1)}, f32[128,512]{1,0:T(8,128)}, u32[]{:S(2)}) copy-start(f32[128,512]{1,0:T(8,128)} %get-tuple-element.28) | copy-start | bytes 786436

commit v2 on v1

--- a/solution.py
+++ b/solution.py
@@ -128,6 +128,8 @@
 MARGIN = 0.3
 SKEW = 0.0
 LEAD = 4.0
+FIRST = 1.0
+SHIP = 16.0
 ZLAG = 0.0
 
 
@@ -186,7 +188,7 @@
         return p if self.kind == FC1 else 1 - p
 
     def sum_home(self, p):
-        if p == 1 and self.index == 1 and self.kind in (FC1, FC2):
+        if self.index == 1 and self.kind in (FC1, FC2):
             return 0 if self.kind == FC1 else 1
         return None
 
@@ -292,16 +294,24 @@
     def own_shard(q):
         return shard(q, r.q_in, r.p_in, r.f1_in, r.f2_in)
 
+    def start_own(q):
+        for p in range(ns):
+            if q.home(p) in (None, p):
+
+                @pl.when(s == p)
+                def _():
+                    target = win(q, wref[q.kind], (p,), a, b, t)
+                    pltpu.make_async_copy(own_shard(q), target, lx.at[q.id, p]).start()
+
     def start_x(q):
         for p in range(ns):
             home = q.home(p)
             target = win(q, wref[q.kind], (p,), a, b, t)
 
-            @pl.when(s == p)
-            def _():
-                if home in (None, p):
-                    pltpu.make_async_copy(own_shard(q), target, lx.at[q.id, p]).start()
-                if home != p:
+            if home != p:
+
+                @pl.when(s == p)
+                def _():
                     send(own_shard(q), target, xs.at[q.id], lx.at[q.id, p], dev(s_=other(p)))
 
             x_at[q.id, p] = plan.clock + 1.0
@@ -525,10 +535,6 @@
     def group_images(g):
         return pl.ds(g * ni, ni)
 
-    pack_small()
-    r.tbl_in[...] = jnp.zeros(r.tbl_in.shape, f32)
-    r.tbl_in[:, 0 : r.v_tab.shape[-1]] = r.v_tab[...]
-
     barrier = pltpu.get_barrier_semaphore()
     peers = (
         [dev(a_=p) for p in a_peers]
@@ -539,6 +545,13 @@
     )
     for p in peers:
         pl.semaphore_signal(barrier, inc=1, device_id=p, device_id_type=MESH)
+    pack_small()
+    r.tbl_in[...] = jnp.zeros(r.tbl_in.shape, f32)
+    r.tbl_in[:, 0 : r.v_tab.shape[-1]] = r.v_tab[...]
+    for q in pieces:
+        start_own(q)
+    for j, src in enumerate((r.images, r.cotangent)):
+        pltpu.make_async_copy(src.at[group_images(t)], r.outb.at[j, t], r.xl.at[j]).start()
     pl.semaphore_wait(barrier, len(peers))
 
     tbl = r.tbl
@@ -550,7 +563,6 @@
         start_x(q)
     xin = r.outb
     for j, src in enumerate((r.images, r.cotangent)):
-        pltpu.make_async_copy(src.at[group_images(t)], xin.at[j, t], r.xl.at[j]).start()
         for k, peer in enumerate(c_peers):
             send(
                 src.at[group_images(peer)],
@@ -722,14 +734,17 @@
         need_small(p)
 
         def ln1(i):
-            n, inv = normalize(X[block(i, rows), :])
-            N1[p, block(i, rows), :] = n.astype(bf16)
-            K[block(i, rows), 2 * p : 2 * p + 1] = inv
+            if p == 0:
+                n = MID[block(i, rows), :]
+            else:
+                n, inv = normalize(X[block(i, rows), :])
+                N1[p, block(i, rows), :] = n.astype(bf16)
+                K[block(i, rows), 2 * p : 2 * p + 1] = inv
             f = (n * row(p, 0) + row(p, 1)).astype(bf16)
             FN[p, block(i, rows), :] = f
             CTX[block(i, NW * WP), :] = dotf(PM[p], f, NN).astype(bf16)
 
-        run(0, ni, 0.45, ln1)
+        run(0, ni, 0.45 if p else 0.25, ln1)
 
         def qkv(c):
             for e in range(nt):
@@ -946,7 +961,7 @@
         if p == 0:
             ship_later(1, p, 1 - p, [first * (i + 1) for i in range(ni)])
         else:
-            ship_later(1, p, 1 - p, [first * ni + 4.0 + 5.0 * i for i in range(ni)])
+            ship_later(1, p, 1 - p, [first * ni + SHIP + 5.0 * i for i in range(ni)])
         run(0, ni * per, cost, image_step)
         run(0, 3, 0.82, qkv_grad, emit_last)
         emit(QKV, p, 2)
@@ -1053,7 +1068,9 @@
 
         @pl.when(s != home)
         def _():
-            send(mine, buffer(6, q), r.s6.at[q.id], r.v6.at[q.id], dev(s_=home))
+            if p == 0:
+                pl.semaphore_wait(r.k6.at[q.id], 1)
+            send(mine, buffer(6, q), r.s6.at[p, q.id], r.v6.at[p, q.id], dev(s_=home))
 
         when = plan.link(f"x{other(home)}", q.unit * na * nb, LINK, HOP)
         plan.add(when, functools.partial(r2x, q, p))
@@ -1062,8 +1079,12 @@
         home = q.sum_home(p)
 
         def body():
-            arrived(buffer(6, q), r.v6.at[q.id])
+            arrived(buffer(6, q), r.v6.at[p, q.id])
             add_into(gwin(q, p, ALL, ALL, t), [buffer(6, q)])
+            if p == 1:
+                pl.semaphore_signal(
+                    r.k6.at[q.id], inc=1, device_id=dev(s_=other(home)), device_id_type=MESH
+                )
 
         on(home, body)
         plan.clock += q.unit * na * nb / 10e6
@@ -1191,7 +1212,7 @@
 
             @pl.when(s != home)
             def _():
-                arrived(gwin(q, p, ALL, ALL, t), r.s6.at[q.id])
+                arrived(gwin(q, p, ALL, ALL, t), r.s6.at[p, q.id])
 
     def add_into(mine, others):
         lead = mine.shape[:-2]
@@ -1291,7 +1312,9 @@
                 max(x_at[after[0].id, after[1]], z_free(*after) - LEAD), functools.partial(next_z, k + 1)
             )
 
-    plan.add(x_at[order[0][0].id, 0], functools.partial(next_z, 0))
+    plan.add(
+        max(x_at[order[0][0].id, 0], z_free(*order[0]) - FIRST), functools.partial(next_z, 0)
+    )
     for q in range(ns):
         arrived(tbl.at[q, t], r.tx.at[q])
         for k, peer in enumerate(c_peers):
@@ -1299,7 +1322,16 @@
     spent(0.5)
     image_ready(0)
     load_rows(0, X)
-    spent(0.3)
+
+    def early_norm(i, carry):
+        n, inv = normalize(X[block(i, rows), :])
+        MID[block(i, rows), :] = n
+        N1[0, block(i, rows), :] = n.astype(bf16)
+        K[block(i, rows), 0:1] = inv
+        return carry
+
+    lax.fori_loop(0, ni, early_norm, 0)
+    spent(1.3)
     for q in range(ns):
         for k, source in enumerate(c_from):
             arrived(tbl.at[q, source], r.tcr.at[q, k])
@@ -1474,8 +1506,9 @@
         v3=dma((2, W)),
         s4=dma((2, W)),
         v4=dma((2, W)),
-        s6=dma((W,)),
-        v6=dma((W,)),
+        s6=dma((2, W)),
+        v6=dma((2, W)),
+        k6=reg((W,)),
         k1=reg((W, nt - 1)),
         k2=reg((W, nb - 1)),
         k3=reg((W,)),

time: 194 us -> 190 us (0.979)
  Pallas kernels: 176 us -> 172 us
    pallas_call x1, Pallas kernels: 176 us -> 172 us  [per_device(): pl.pallas_call(functools.partial(kernel, z), out_shape=tuple((o for o, _...]
where the time goes in v2:
time: 190 us
  Pallas kernels  172 us (91%)
  local copies, waits for them, and re-layouts  17 us (9%)
    pallas_call x1, Pallas kernels, per_device(): pl.pallas_call(functools.partial(kernel, z), out_shape=tuple((o for o, _...  172 us
    unnamed x22, local copies, waits for them, and re-layouts  11.4 us

profile of v2, /device:TPU:0, one launch (start us, length us, event | category | flops | bytes accessed | tf_op | source)
XLA Modules:
  0.0 189.8 jit_solution(11480737434178537614)
XLA Ops:
  0.7 1.5 constant_dynamic-slice_fusion.2
  2.1 1.1 copy.37.refs_0_
  3.3 1.1 copy.38.refs_1_
  4.4 172.1 %two_blocks.1 = (bf16[16,98,512]{2,1,0:T(8,128)(2,1)}, bf16[16,98,512]{2,1,0:T(8,128)(2,1)}, f32[3,64,256]{2,1,0:T(8,128)}, f32[32,512]{1,0:T(8,128)}, f32[64,10...) custom-call(bf16[8,98,512]{2,1,0:T(8,128)(2,1)} %copy.37.refs_0_, ...), custom_call_target="tpu_custom_call" | custom-call | tf_op jit(solution)/shard_map/two_blocks/pallas_call | solution.py:1527
  176.5 0.7 slice_bitcast_fusion
  177.2 0.5 constant_dynamic-slice_fusion
  177.7 0.8 dynamic-slice_bitcast_fusion
  178.5 0.6 copy.36
  179.1 1.5 constant_dynamic-slice_fusion.4
  180.6 0.7 constant_dynamic-slice_fusion.8
  181.3 0.1 reverse
  181.4 0.7 slice_bitcast_fusion.1
  182.1 0.0 copy-start
  182.1 3.2 %copy.34 = bf16[1,16,98,512]{3,1,2,0:T(8,128)(2,1)} copy(bf16[1,16,98,512]{3,2,1,0:T(8,128)(2,1)} %bitcast.30) | data formatting | bytes 3211264
  185.3 0.0 copy-done
  185.3 0.0 copy-start.3
  185.3 0.0 copy-start.4
  185.3 0.0 copy-start.2
  185.3 0.0 copy-start.1
  185.4 1.7 copy.35
  187.0 0.0 copy-done.3
  187.0 0.7 copy.44
  187.7 0.0 copy-done.4
  187.7 0.6 copy.45
  188.3 0.0 copy-done.2
  188.3 0.7 copy.46
  189.0 0.0 copy-done.1
  189.0 0.7 copy.47
  (1 shorter events, 0.0 us)
Async XLA Ops:
  182.1 3.2 %copy-start = (bf16[16,98,512]{2,1,0:T(8,128)(2,1)S(1)}, bf16[16,98,512]{2,1,0:T(8,128)(2,1)}, u32[]{:S(2)}) copy-start(bf16[16,98,512]{2,1,0:T(8,128)(2,1)} %get-tuple-element.23) | copy-start | bytes 4816900
  185.3 1.7 copy-start.3
  185.3 2.4 %copy-start.4 = (f32[32,512]{1,0:T(8,128)S(1)}, f32[32,512]{1,0:T(8,128)}, u32[]{:S(2)}) copy-start(f32[32,512]{1,0:T(8,128)} %get-tuple-element.26) | copy-start | bytes 196612
  185.3 3.0 %copy-start.2 = (f32[64,1024]{1,0:T(8,128)S(1)}, f32[64,1024]{1,0:T(8,128)}, u32[]{:S(2)}) copy-start(f32[64,1024]{1,0:T(8,128)} %get-tuple-element.27) | copy-start | bytes 786436
  185.3 3.7 %copy-start.1 = (f32[128,512]{1,0:T(8,128)S(1)}, f32[128,512]{1,0:T(8,128)}, u32[]{:S(2)}) copy-start(f32[128,512]{1,0:T(8,128)} %get-tuple-element.28) | copy-start | bytes 786436

commit v3 on v2

--- a/solution.py
+++ b/solution.py
@@ -123,7 +123,7 @@
 
 LINK = 90.0e3
 CORE_LINK = 430.0e3
-HOP = 2.0
+HOP = 2.3
 CORE_HOP = 0.8
 MARGIN = 0.3
 SKEW = 0.0

time: 190 us -> 189 us (level)
  no operation moved by 1% of the time
where the time goes in v3:
time: 189 us
  Pallas kernels  171 us (90%)
  local copies, waits for them, and re-layouts  17 us (9%)
    pallas_call x1, Pallas kernels, per_device(): pl.pallas_call(functools.partial(kernel, z), out_shape=tuple((o for o, _...  171 us
    unnamed x22, local copies, waits for them, and re-layouts  11.4 us

profile of v3, /device:TPU:0, one launch (start us, length us, event | category | flops | bytes accessed | tf_op | source)
XLA Modules:
  0.0 189.0 jit_solution(5489233125611210516)
XLA Ops:
  0.7 1.5 constant_dynamic-slice_fusion.2
  2.1 1.1 copy.37.refs_0_
  3.3 1.1 copy.38.refs_1_
  4.4 171.3 %two_blocks.1 = (bf16[16,98,512]{2,1,0:T(8,128)(2,1)}, bf16[16,98,512]{2,1,0:T(8,128)(2,1)}, f32[3,64,256]{2,1,0:T(8,128)}, f32[32,512]{1,0:T(8,128)}, f32[64,10...) custom-call(bf16[8,98,512]{2,1,0:T(8,128)(2,1)} %copy.37.refs_0_, ...), custom_call_target="tpu_custom_call" | custom-call | tf_op jit(solution)/shard_map/two_blocks/pallas_call | solution.py:1527
  175.7 0.7 slice_bitcast_fusion
  176.5 0.5 constant_dynamic-slice_fusion
  177.0 0.8 dynamic-slice_bitcast_fusion
  177.7 0.6 copy.36
  178.3 1.5 constant_dynamic-slice_fusion.4
  179.8 0.7 constant_dynamic-slice_fusion.8
  180.5 0.1 reverse
  180.7 0.7 slice_bitcast_fusion.1
  181.3 0.0 copy-start
  181.3 3.2 %copy.34 = bf16[1,16,98,512]{3,1,2,0:T(8,128)(2,1)} copy(bf16[1,16,98,512]{3,2,1,0:T(8,128)(2,1)} %bitcast.30) | data formatting | bytes 3211264
  184.6 0.0 copy-done
  184.6 0.0 copy-start.3
  184.6 0.0 copy-start.4
  184.6 0.0 copy-start.2
  184.6 0.0 copy-start.1
  184.6 1.7 copy.35
  186.3 0.0 copy-done.3
  186.3 0.7 copy.44
  186.9 0.0 copy-done.4
  186.9 0.6 copy.45
  187.6 0.0 copy-done.2
  187.6 0.7 copy.46
  188.3 0.0 copy-done.1
  188.3 0.7 copy.47
  (1 shorter events, 0.0 us)
Async XLA Ops:
  181.3 3.2 %copy-start = (bf16[16,98,512]{2,1,0:T(8,128)(2,1)S(1)}, bf16[16,98,512]{2,1,0:T(8,128)(2,1)}, u32[]{:S(2)}) copy-start(bf16[16,98,512]{2,1,0:T(8,128)(2,1)} %get-tuple-element.23) | copy-start | bytes 4816900
  184.6 1.7 copy-start.3
  184.6 2.4 %copy-start.4 = (f32[32,512]{1,0:T(8,128)S(1)}, f32[32,512]{1,0:T(8,128)}, u32[]{:S(2)}) copy-start(f32[32,512]{1,0:T(8,128)} %get-tuple-element.26) | copy-start | bytes 196612
  184.6 3.0 %copy-start.2 = (f32[64,1024]{1,0:T(8,128)S(1)}, f32[64,1024]{1,0:T(8,128)}, u32[]{:S(2)}) copy-start(f32[64,1024]{1,0:T(8,128)} %get-tuple-element.27) | copy-start | bytes 786436
  184.6 3.7 %copy-start.1 = (f32[128,512]{1,0:T(8,128)S(1)}, f32[128,512]{1,0:T(8,128)}, u32[]{:S(2)}) copy-start(f32[128,512]{1,0:T(8,128)} %get-tuple-element.28) | copy-start | bytes 786436
